TPU v7x, 32 devices: a whole 2x2x4 slice. The times are simulated.
32 devices in a mesh: dp: 8 (over y, x, core), mp: 4 (over z).
Axes of the slice: x: 2, y: 2, z: 4, core: 2. Of those that a mesh axis runs over, the one named last changes fastest.
Arguments:
- img_tokens: bfloat16 [32, 128, 1408], P(('dp', 'mp')), may hold values from -6 to 6
- w_key: bfloat16 [1408, 2048], P(None, 'mp'), may hold values from -0.15625 to 0.15625
- w_value: bfloat16 [1408, 2048], P(None, 'mp'), may hold values from -0.15625 to 0.15625
- queries: bfloat16 [32, 32, 2048], P('dp', None, 'mp'), may hold values from -6 to 6
- lengths: int32 [32], P('dp'), may hold values from 1 to 32
- d_out: bfloat16 [32, 32, 2048], P('dp', None, 'mp'), may hold values from -6 to 6
- img_pooled: bfloat16 [32, 1408], P(('dp', 'mp')), may hold values from -40 to 40
- w_proj: bfloat16 [1408, 2048], P(None, 'mp'), may hold values from -0.19921875 to 0.19921875
- txt_embed: bfloat16 [32, 2048], P('dp', 'mp'), may hold values from -80 to 80
- inv_temp: float32 [1], replicated, may hold values from 30 to 100
Outputs:
- attended: bfloat16 [32, 32, 2048], P('dp', None, 'mp')
- grad_queries: bfloat16 [32, 32, 2048], P('dp', None, 'mp')
- dw_key: float32 [1408, 2048], P('dp', 'mp')
- dw_value: float32 [1408, 2048], P('dp', 'mp')
- contrast: float32 [2, 32], P(None, 'dp')
Inputs may be any that keep to these rules, and one draw needn't show every extreme that they name: lengths: each caption's count of real positions.
All inputs are finite; a program needn't handle non-finite values.
Results may differ from a plain program's by a relative error of at most 0.0081.
Values may be sent and summed in bfloat16 or wider, within the bound.
No kernel may reach another device: no remote copies, remote signals or barrier semaphores. Data moves between devices by JAX's collectives and lax.ppermute only.
A program may use at most 64 MiB of HBM per device.

v0:
```python
import functools

import jax
import jax.numpy as jnp
from jax import lax
from jax.experimental import pallas as pl
from jax.experimental.pallas import tpu as pltpu
from jax.sharding import PartitionSpec as P


HD = 128
F32 = jnp.float32
BF16 = jnp.bfloat16


def dot(a, b, ca, cb):
    return lax.dot_general(a, b, (((ca,), (cb,)), ((), ())), preferred_element_type=F32)


def pick(ready, choices, store):
    if len(choices) == 1:
        store[...] = choices[0][0]
        return

    @pl.when(ready == 1)
    def _():
        store[...] = choices[0][0]

    @pl.when(ready == 0)
    def _():
        store[...] = choices[1][0]


def group_kernel(heads, counts, flags, lens, *refs):
    n = len(counts)
    inputs, rest = refs[: sum(counts)], refs[sum(counts) :]
    wk, wv, qs, dos, att, gq, grads, kept, sent, store, turned = rest
    inv = HD ** (-0.5)
    width = heads * HD
    image_len = store.shape[0] // n
    core = flags[2 * n]
    spans = [slice(s * image_len, (s + 1) * image_len) for s in range(n)]
    at = 0
    for s, count in enumerate(counts):
        pick(flags[s], inputs[at : at + count], store.at[spans[s]])
        at += count
    x = store[...]
    keys = jnp.dot(x, wk[...], preferred_element_type=F32).astype(BF16)
    values = jnp.dot(x, wv[...], preferred_element_type=F32).astype(BF16)
    rows, half = turned.shape[1], turned.shape[0] // 2
    for s in range(n):
        flipped = x[spans[s]].T
        for m in range(2 * half):
            turned[m] = flipped[m * rows : (m + 1) * rows]
        for m in range(half):
            kept[s, m] = turned[2 * m + core]
            sent[s, m] = turned[2 * m + 1 - core]
    cols = [slice(h * HD, (h + 1) * HD) for h in range(heads)]
    pairs = [(s, c) for s in range(n) for c in cols]
    keep = []
    for s in range(n):
        length = lens[flags[n + s]]
        at_row = lax.broadcasted_iota(jnp.int32, (qs.shape[1], HD), 0)
        keep.append((at_row < length).astype(F32))
    k = [keys[spans[s], c] for s, c in pairs]
    v = [values[spans[s], c] for s, c in pairs]
    q = [qs[flags[n + s], :, c] for s, c in pairs]
    masked = [(dos[flags[n + s], :, c].astype(F32) * keep[s]).astype(BF16) for s, c in pairs]
    scores = [dot(a, b, 1, 1) * inv for a, b in zip(q, k)]
    grad_probs = [dot(a, b, 1, 1) for a, b in zip(masked, v)]
    tops = [jnp.max(s, axis=1, keepdims=True) for s in scores]
    exps = [jnp.exp(s - t) for s, t in zip(scores, tops)]
    probs = [e / jnp.sum(e, axis=1, keepdims=True) for e in exps]
    probs_b = [p.astype(BF16) for p in probs]
    row_dots = [jnp.sum(p * g, axis=1, keepdims=True) for p, g in zip(probs, grad_probs)]
    grad_scores = [
        (p * (g - r) * inv).astype(BF16) for p, g, r in zip(probs, grad_probs, row_dots)
    ]
    for i, (s, c) in enumerate(pairs):
        other = slice(width + c.start, width + c.stop)
        grads[spans[s], c] = dot(grad_scores[i], q[i], 0, 0).astype(BF16)
        grads[spans[s], other] = dot(probs_b[i], masked[i], 0, 0).astype(BF16)
        att[s, :, c] = (dot(probs_b[i], v[i], 1, 0) * keep[s]).astype(BF16)
        gq[s, :, c] = dot(grad_scores[i], k[i], 1, 0).astype(BF16)


def image_group(flags, lengths, choices, n_dp, w_key, w_value, queries, d_out):
    n = len(choices)
    caption_len, width = queries.shape[1:]
    image_len, feats = choices[0][0].shape[1:]
    rows, half = feats // n_dp, n_dp // 2
    flat = [c for several in choices for c in several]
    shapes = [
        (n, caption_len, width),
        (n, caption_len, width),
        (n * image_len, 2 * width),
        (n, half, rows, image_len),
        (n, half, rows, image_len),
    ]
    full = lambda shape: pl.BlockSpec(shape, lambda i, a, b: (0,) * len(shape))
    operands = [*flat, w_key, w_value, queries, d_out]
    return pl.pallas_call(
        functools.partial(group_kernel, width // HD, [len(c) for c in choices]),
        grid_spec=pltpu.PrefetchScalarGridSpec(
            num_scalar_prefetch=2,
            grid=(1,),
            in_specs=[full(o.shape) for o in operands],
            out_specs=[full(s) for s in shapes],
            scratch_shapes=[
                pltpu.VMEM((n * image_len, feats), BF16),
                pltpu.VMEM((n_dp, rows, image_len), BF16),
            ],
        ),
        out_shape=[jax.ShapeDtypeStruct(s, BF16) for s in shapes],
        compiler_params=pltpu.CompilerParams(vmem_limit_bytes=20 * 2**20),
        name="image_group",
    )(flags, lengths, *operands)


def terms_kernel(count, pieces, order, *refs):
    turned, grads, outs = refs[:count], refs[count : 2 * count], refs[2 * count :]
    right = jnp.concatenate([g[...] for g in grads], axis=0)
    for piece, out in zip(pieces, outs):
        place = order[piece]
        left = jnp.concatenate([t[s, place] for t in turned for s in range(t.shape[0])], axis=1)
        out[...] = jnp.dot(left, right, preferred_element_type=F32).astype(out.dtype)


def weight_terms(order, pieces, turned, grads):
    count = len(turned)
    rows, width = turned[0].shape[2], grads[0].shape[1]
    full = lambda shape: pl.BlockSpec(shape, lambda i, o: (0,) * len(shape))
    return pl.pallas_call(
        functools.partial(terms_kernel, count, pieces),
        grid_spec=pltpu.PrefetchScalarGridSpec(
            num_scalar_prefetch=1,
            grid=(1,),
            in_specs=[full(o.shape) for o in (*turned, *grads)],
            out_specs=[full((rows, width))] * len(pieces),
        ),
        out_shape=[
            jax.ShapeDtypeStruct((rows, width), F32 if piece == 0 else BF16) for piece in pieces
        ],
        compiler_params=pltpu.CompilerParams(vmem_limit_bytes=20 * 2**20),
        name="weight_terms",
    )(order, *turned, *grads)


def finish_kernel(*refs):
    own, arrived, outs = refs[0], refs[1:-2], refs[-2:]
    width = outs[0].shape[1]
    for side, out in enumerate(outs):
        cols = slice(side * width, (side + 1) * width)
        total = own[:, cols]
        for piece in arrived:
            total = total + piece[:, cols].astype(F32)
        out[...] = total


def finish(own, arrived):
    rows, width = own.shape
    shape = jax.ShapeDtypeStruct((rows, width // 2), F32)
    return pl.pallas_call(
        finish_kernel,
        out_shape=[shape, shape],
        compiler_params=pltpu.CompilerParams(vmem_limit_bytes=12 * 2**20),
        name="finish",
    )(own, *arrived)


def arrange_kernel(slots, place, *refs):
    count = len(slots)
    at = 0
    for g, several in enumerate(slots):
        for s in range(several):
            for side in range(2):
                refs[2 * count + side][place[at]] = refs[2 * g + side][s]
            at += 1


def arrange(images, parts, slots):
    shape = (sum(slots), *parts[0].shape[1:])
    full = lambda shape: pl.BlockSpec(shape, lambda i, o: (0,) * len(shape))
    return pl.pallas_call(
        functools.partial(arrange_kernel, slots),
        grid_spec=pltpu.PrefetchScalarGridSpec(
            num_scalar_prefetch=1,
            grid=(1,),
            in_specs=[full(p.shape) for p in parts],
            out_specs=[full(shape)] * 2,
        ),
        out_shape=[jax.ShapeDtypeStruct(shape, BF16)] * 2,
        compiler_params=pltpu.CompilerParams(vmem_limit_bytes=12 * 2**20),
        name="arrange",
    )(images, *parts)


def facts_kernel(pooled, texts, out):
    feats, width = pooled.shape[1], texts.shape[1]
    out[:, :feats] = pooled[...]
    for c in range(texts.shape[0]):
        out[:, feats + c * width : feats + (c + 1) * width] = texts[c : c + 1, :]


def join_facts(pooled, texts):
    return pl.pallas_call(
        facts_kernel,
        out_shape=jax.ShapeDtypeStruct((1, pooled.shape[1] + texts.size), BF16),
        compiler_params=pltpu.CompilerParams(vmem_limit_bytes=2 * 2**20),
        name="join_facts",
    )(pooled, texts)


def sims_kernel(place, *refs):
    facts, (w_proj, out, rows, texts) = refs[:-4], refs[-4:]
    n_dp = facts[0].shape[0]
    feats, width = w_proj.shape
    captions = texts.shape[0] // n_dp
    for r, piece in enumerate(facts):
        start = pl.multiple_of((place[0] ^ r) * n_dp, n_dp)
        rows[pl.ds(start, n_dp)] = piece[:, :feats].astype(F32)
    for c in range(captions):
        texts[c * n_dp : (c + 1) * n_dp] = facts[0][
            :, feats + c * width : feats + (c + 1) * width
        ].astype(F32)
    img_raw = jnp.dot(
        rows[...].astype(BF16), w_proj[...], preferred_element_type=F32
    ).astype(BF16)
    txt = texts[...]
    raw = img_raw.astype(F32)
    count = txt.shape[0]
    out[:, :count] = dot(img_raw, txt.astype(BF16), 1, 1)
    out[:, count : count + 1] = jnp.sum(raw * raw, axis=1, keepdims=True)
    out[:, count + 1 : count + 2] = jnp.sum(txt * txt, axis=1, keepdims=True)


def similarity_terms(place, facts, w_proj, captions):
    n_dp = facts[0].shape[0]
    count, feats = n_dp * len(facts), w_proj.shape[0]
    full = lambda shape: pl.BlockSpec(shape, lambda i, o: (0,) * len(shape))
    return pl.pallas_call(
        sims_kernel,
        grid_spec=pltpu.PrefetchScalarGridSpec(
            num_scalar_prefetch=1,
            grid=(1,),
            in_specs=[full(o.shape) for o in (*facts, w_proj)],
            out_specs=full((count, n_dp * captions + 2)),
            scratch_shapes=[
                pltpu.VMEM((count, feats), F32),
                pltpu.VMEM((n_dp * captions, w_proj.shape[1]), F32),
            ],
        ),
        out_shape=jax.ShapeDtypeStruct((count, n_dp * captions + 2), F32),
        compiler_params=pltpu.CompilerParams(vmem_limit_bytes=16 * 2**20),
        name="similarity_terms",
    )(place, *facts, w_proj)


def losses_kernel(n_dp, place, *refs):
    inv_temp, terms, (out, store) = refs[0], refs[1:-2], refs[-2:]
    for r, term in enumerate(terms):
        store[place[0] ^ r] = term[...]
    total = store[0]
    for r in range(1, len(terms)):
        total = total + store[r]
    count = total.shape[0]
    captions = out.shape[1]
    img_sq = total[:, count : count + 1]
    txt_sq = jnp.broadcast_to(total[:, count + 1 : count + 2], (count, HD)).T[0:1, :]
    scale = inv_temp[0]
    logits = scale * total[:, :count] * lax.rsqrt(img_sq + 1e-06) * lax.rsqrt(txt_sq + 1e-06)
    row_top = jnp.max(logits, axis=1, keepdims=True)
    row_lse = row_top + jnp.log(jnp.sum(jnp.exp(logits - row_top), axis=1, keepdims=True))
    col_top = jnp.max(logits, axis=0, keepdims=True)
    col_lse = col_top + jnp.log(jnp.sum(jnp.exp(logits - col_top), axis=0, keepdims=True))
    row = lax.broadcasted_iota(jnp.int32, (count, HD), 0)
    lane = lax.broadcasted_iota(jnp.int32, (count, HD), 1)
    mine = (row == lane * n_dp) & (lane < captions)
    grid_row = lax.broadcasted_iota(jnp.int32, (count, count), 0)
    grid_col = lax.broadcasted_iota(jnp.int32, (count, count), 1)
    diag = jnp.sum(jnp.where(grid_row == grid_col, logits, 0.0), axis=1, keepdims=True)
    image_side = jnp.sum(jnp.where(mine, row_lse - diag, 0.0), axis=0, keepdims=True)
    col_lse = jnp.sum(jnp.where(grid_row == grid_col, col_lse, 0.0), axis=1, keepdims=True)
    caption_side = jnp.sum(jnp.where(mine, col_lse - diag, 0.0), axis=0, keepdims=True)
    out[0:1, :] = image_side[:, :captions]
    out[1:2, :] = caption_side[:, :captions]


def large_losses(place, inv_temp, terms, n_dp):
    count = terms[0].shape[0]
    stacked = jnp.stack(terms)
    total = stacked[place[0] ^ 0]
    for z in range(1, len(terms)):
        total = total + stacked[place[0] ^ z]
    img_sq, txt_sq = total[:, count], total[:, count + 1]
    logits = (
        inv_temp[0]
        * total[:, :count]
        * lax.rsqrt(img_sq + 1e-06)[:, None]
        * lax.rsqrt(txt_sq + 1e-06)[None, :]
    )
    diag = jnp.diagonal(logits)[::n_dp]
    image_side = jax.nn.logsumexp(logits[::n_dp], axis=1) - diag
    caption_side = jax.nn.logsumexp(logits[:, ::n_dp], axis=0) - diag
    return jnp.stack([image_side, caption_side])


def losses(place, inv_temp, terms, n_dp, captions):
    shape = terms[0].shape
    if shape[0] > HD:
        return large_losses(place, inv_temp, terms, n_dp)
    full = lambda shape: pl.BlockSpec(shape, lambda i, o: (0,) * len(shape))
    return pl.pallas_call(
        functools.partial(losses_kernel, n_dp),
        grid_spec=pltpu.PrefetchScalarGridSpec(
            num_scalar_prefetch=1,
            grid=(1,),
            in_specs=[pl.BlockSpec(memory_space=pltpu.SMEM)] + [full(shape)] * len(terms),
            out_specs=full((2, captions)),
            scratch_shapes=[pltpu.VMEM((len(terms), *shape), F32)],
        ),
        out_shape=jax.ShapeDtypeStruct((2, captions), F32),
        compiler_params=pltpu.CompilerParams(vmem_limit_bytes=40 * 2**20),
        name="losses",
    )(place, inv_temp, *terms)


def flip(array, axis, count, mask):
    return lax.ppermute(array, axis, [(n, n ^ mask) for n in range(count)])


def body(n_dp, n_mp, *args):
    return work(n_dp, n_mp, *args)


def slot_groups(n_mp):
    return [[0], [1, n_mp - 1]] + [[s] for s in range(n_mp - 2, 1, -1)]


def work(
    n_dp,
    n_mp,
    img_tokens,
    w_key,
    w_value,
    queries,
    lengths,
    d_out,
    img_pooled,
    w_proj,
    txt_embed,
    inv_temp,
):
    group = lax.axis_index("dp").astype(jnp.int32)
    place = lax.axis_index("mp").astype(jnp.int32)
    captions = queries.shape[0]

    right, left = {0: img_tokens}, {0: img_tokens}
    for d in range(1, n_mp - 1):
        ups = [(n, n + 1) for n in range(d - 1, n_mp - 1)]
        downs = [(n_mp - 1 - a, n_mp - 1 - b) for a, b in ups]
        right[d] = lax.ppermute(right[d - 1], "mp", ups)
        left[d] = lax.ppermute(left[d - 1], "mp", downs)
        if d == 1:
            ends = [(0, n_mp - 1), (n_mp - 1, 0)]
            right[n_mp - 1] = left[n_mp - 1] = lax.ppermute(img_tokens, "mp", ends)

    facts = join_facts(img_pooled, txt_embed)
    mask = 1
    while mask < n_dp:
        facts = jnp.concatenate([facts, flip(facts, "dp", n_dp, mask)], axis=0)
        mask *= 2

    core = group % 2
    parts, turned, others, grads, other_grads, images = [], [], [], [], [], []
    groups = slot_groups(n_mp)
    for slots in groups:
        choices = [[right[s], left[n_mp - s]] if s else [img_tokens] for s in slots]
        here = [(place - s) % n_mp for s in slots]
        images += here
        flags = jnp.stack([(place >= s).astype(jnp.int32) for s in slots] + here + [core])
        att, gq, grad, kept, sent = image_group(
            flags, lengths, choices, n_dp, w_key, w_value, queries, d_out
        )
        parts += [att, gq]
        turned.append(kept)
        others.append(flip(sent, "dp", n_dp, 1))
        grads.append(grad)
        other_grads.append(flip(grad, "dp", n_dp, 1))

    half = n_dp // 2
    order = ((group // 2) ^ jnp.arange(half)).astype(jnp.int32)
    sides = (turned + others, grads + other_grads)
    (last,) = weight_terms(order, (half - 1,), *sides)
    arrived = [flip(last, "dp", n_dp, 2 * (half - 1))]
    pieces = weight_terms(order, tuple(range(half - 2, -1, -1)), *sides)
    for m, piece in zip(range(half - 2, 0, -1), pieces):
        arrived.append(flip(piece, "dp", n_dp, 2 * m))
    attended, grad_queries = arrange(jnp.stack(images), parts, [len(s) for s in groups])
    dw_key, dw_value = finish(pieces[-1], arrived)

    pools = [facts] + [flip(facts, "mp", n_mp, m) for m in range(1, n_mp)]
    spot = place.reshape(1)
    terms = similarity_terms(spot, pools, w_proj, captions)
    terms = [terms] + [flip(terms, "mp", n_mp, m) for m in range(1, n_mp)]
    contrast = losses(spot, inv_temp, terms, n_dp, captions)
    return (attended, grad_queries, dw_key, dw_value, contrast)


def solution(mesh):
    placed = (
        P(("dp", "mp"), None, None),
        P(None, "mp"),
        P(None, "mp"),
        P("dp", None, "mp"),
        P("dp"),
        P("dp", None, "mp"),
        P(("dp", "mp"), None),
        P(None, "mp"),
        P("dp", "mp"),
        P(),
    )
    n_dp, n_mp = mesh.shape["dp"], mesh.shape["mp"]
    return jax.shard_map(
        functools.partial(body, n_dp, n_mp),
        mesh=mesh,
        in_specs=placed,
        out_specs=(
            P("dp", None, "mp"),
            P("dp", None, "mp"),
            P("dp", "mp"),
            P("dp", "mp"),
            P(None, "dp"),
        ),
        check_vma=False,
    )
```

profile of v0, /device:TPU:0, one launch (start us, length us, event | category | flops | bytes accessed | tf_op | source)
XLA Modules:
  0.0 79.8 jit_solution(16893367557728650327)
XLA Ops:
  0.6 5.7 %collective-permute-start = (bf16[1,128,1408]{2,1,0:T(8,128)(2,1)}, bf16[1,128,1408]{2,1,0:T(8,128)(2,1)}, u32[]{:S(2)}, u32[]{:S(2)}) collective-permute-start(bf16[1,128,1408]{2,1,0:T(8,128)(2,1)} %refs_0_.2), channel_id=1, source_target_pairs={{0,1},{1,2},{2,3},{4,5},{5,6},{6,7},{8,9},{9,10},{10,11},{12,13},{... | collective-permute-start | bytes 1081352 | tf_op jit(solution)/shard_map/ppermute | solution.py:362
  6.3 1.3 %collective-permute-start.2 = (bf16[1,128,1408]{2,1,0:T(8,128)(2,1)}, bf16[1,128,1408]{2,1,0:T(8,128)(2,1)}, u32[]{:S(2)}, u32[]{:S(2)}) collective-permute-start(bf16[1,128,1408]{2,1,0:T(8,128)(2,1)} %refs_0_.2), channel_id=1, source_target_pairs={{3,2},{2,1},{1,0},{7,6},{6,5},{5,4},{11,10},{10,9},{9,8},{15,14},{... | collective-permute-start | bytes 1081352 | tf_op jit(solution)/shard_map/ppermute | solution.py:363
  7.6 6.6 %collective-permute-start.1 = (bf16[1,128,1408]{2,1,0:T(8,128)(2,1)}, bf16[1,128,1408]{2,1,0:T(8,128)(2,1)S(1)}, u32[]{:S(2)}, u32[]{:S(2)}) collective-permute-start(bf16[1,128,1408]{2,1,0:T(8,128)(2,1)} %refs_0_.2), channel_id=1, source_target_pairs={{0,3},{3,0},{4,7},{7,4},{8,11},{11,8},{12,15},{15,12},{16,19},{19,... | collective-permute-start | bytes 1081352 | tf_op jit(solution)/shard_map/ppermute | solution.py:366
  15.8 1.4 %copy-done = bf16[1408,512]{1,0:T(8,128)(2,1)S(1)} copy-done((bf16[1408,512]{1,0:T(8,128)(2,1)S(1)}, bf16[1408,512]{1,0:T(8,128)(2,1)}, u32[]{:S(2)}) %copy-start) | copy-done | bytes 1441816
  17.2 1.4 %copy-done.2 = bf16[1408,512]{1,0:T(8,128)(2,1)S(1)} copy-done((bf16[1408,512]{1,0:T(8,128)(2,1)S(1)}, bf16[1408,512]{1,0:T(8,128)(2,1)}, u32[]{:S(2)}) %copy-start.2) | copy-done | bytes 1441816
  18.5 0.9 %copy-done.5 = bf16[4,32,512]{2,1,0:T(8,128)(2,1)S(1)} copy-done((bf16[4,32,512]{2,1,0:T(8,128)(2,1)S(1)}, bf16[4,32,512]{2,1,0:T(8,128)(2,1)}, u32[]{:S(2)}) %copy-start.5) | copy-done | bytes 131096
  19.4 0.9 %copy-done.7 = bf16[4,32,512]{2,1,0:T(8,128)(2,1)S(1)} copy-done((bf16[4,32,512]{2,1,0:T(8,128)(2,1)S(1)}, bf16[4,32,512]{2,1,0:T(8,128)(2,1)}, u32[]{:S(2)}) %copy-start.7) | copy-done | bytes 131096
  20.4 1.0 %copy-done.13 = bf16[1,128,1408]{2,1,0:T(8,128)(2,1)S(1)} copy-done((bf16[1,128,1408]{2,1,0:T(8,128)(2,1)S(1)}, bf16[1,128,1408]{2,1,0:T(8,128)(2,1)}, u32[]{:S(2)}) %copy-start.13) | copy-done | bytes 360472
  22.0 2.4 %image_group.3 = (bf16[1,32,512]{2,1,0:T(8,128)(2,1)S(1)}, bf16[1,32,512]{2,1,0:T(8,128)(2,1)S(1)}, bf16[128,1024]{1,0:T(8,128)(2,1)S(1)}, bf16[1,4,176,128]{3,2,1,0:T(8,128)(2,1)S(1)}, bf16[1,4,176,128]{3,2,1,0:T(8,128)(2,1)}) custom-call(s32[3]{0:T(128)S(1)} %add_add_fusion.flags, s32[4]{0:T(128)S(1)} %copy-done.17, bf16[1,128,1408]{2,1,0:T(8,128)(2,1)S(1)} %copy-done.13, ...), custom_call_target="tpu_custom_call" | custom-call | tf_op jit(solution)/shard_map/image_group/pallas_call | solution.py:102
  26.9 1.4 %collective-permute-start.3 = (bf16[1,128,1408]{2,1,0:T(8,128)(2,1)}, bf16[1,128,1408]{2,1,0:T(8,128)(2,1)}, u32[]{:S(2)}, u32[]{:S(2)}) collective-permute-start(bf16[1,128,1408]{2,1,0:T(8,128)(2,1)} %collective-permute-done.refs_0_), channel_id=1, source_target_pairs={{1,2},{2,3},{5,6},{6,7},{9,10},{10,11},{13,14},{14,15},{17,18},{18... | collective-permute-start | bytes 1081352 | tf_op jit(solution)/shard_map/ppermute | solution.py:362
  28.3 1.3 %collective-permute-start.4 = (bf16[1,128,1408]{2,1,0:T(8,128)(2,1)}, bf16[1,128,1408]{2,1,0:T(8,128)(2,1)}, u32[]{:S(2)}, u32[]{:S(2)}) collective-permute-start(bf16[1,128,1408]{2,1,0:T(8,128)(2,1)} %collective-permute-done.2.refs_3_), channel_id=1, source_target_pairs={{2,1},{1,0},{6,5},{5,4},{10,9},{9,8},{14,13},{13,12},{18,17},{17,1... | collective-permute-start | bytes 1081352 | tf_op jit(solution)/shard_map/ppermute | solution.py:363
  29.6 1.3 %pad_maximum_fusion.2 = bf16[2,3456]{1,0:T(2,128)(2,1)} fusion(bf16[1,3456]{1,0:T(2,128)(2,1)} %collective-permute-done.14, bf16[1,3456]{1,0:T(2,128)(2,1)S(1)} %join_facts.1), kind=kLoop, calls=%fused_computation.2 | loop fusion | flops 27648 | bytes 27648 | tf_op jit(solution)/shard_map/concatenate | solution.py:371
  30.9 1.5 %collective-permute-start.15 = (bf16[2,3456]{1,0:T(2,128)(2,1)}, bf16[2,3456]{1,0:T(2,128)(2,1)}, u32[]{:S(2)}, u32[]{:S(2)}) collective-permute-start(bf16[2,3456]{1,0:T(2,128)(2,1)} %pad_maximum_fusion.2), channel_id=1, source_target_pairs={{0,8},{4,12},{8,0},{12,4},{16,24},{20,28},{24,16},{28,20},{1,9},{5... | collective-permute-start | bytes 41480 | tf_op jit(solution)/shard_map/ppermute | solution.py:329
  35.0 3.5 %image_group.4 = (bf16[2,32,512]{2,1,0:T(8,128)(2,1)S(1)}, bf16[2,32,512]{2,1,0:T(8,128)(2,1)S(1)}, bf16[256,1024]{1,0:T(8,128)(2,1)S(1)}, bf16[2,4,176,128]{3,2...) custom-call(s32[5]{0:T(128)S(1)} %copy-done.22, s32[4]{0:T(128)S(1)} %copy-done.18, ...), custom_call_target="tpu_custom_call" | custom-call | tf_op jit(solution)/shard_map/image_group/pallas_call | solution.py:102
  39.0 1.8 %collective-permute-done.4.refs_1_ = bf16[1,128,1408]{2,1,0:T(8,128)(2,1)} collective-permute-done((bf16[1,128,1408]{2,1,0:T(8,128)(2,1)}, bf16[1,128,1408]{2,1,0:T(8,128)(2,1)}, u32[]{:S(2)}, u32[]{:S(2)}) %collective-permute-start.4) | collective-permute-done | bytes 360480 | tf_op jit(solution)/shard_map/ppermute | solution.py:363
  40.8 2.8 %image_group.5 = (bf16[1,32,512]{2,1,0:T(8,128)(2,1)S(1)}, bf16[1,32,512]{2,1,0:T(8,128)(2,1)S(1)}, bf16[128,1024]{1,0:T(8,128)(2,1)S(1)}, bf16[1,4,176,128]{3,2...) custom-call(s32[3]{0:T(128)S(1)} %copy-done.21, s32[4]{0:T(128)S(1)} %copy-done.19, ...), custom_call_target="tpu_custom_call" | custom-call | tf_op jit(solution)/shard_map/image_group/pallas_call | solution.py:102
  44.3 0.8 pad_maximum_fusion.1
  45.1 1.6 %collective-permute-start.16 = (bf16[4,3456]{1,0:T(4,128)(2,1)S(1)}, bf16[4,3456]{1,0:T(4,128)(2,1)S(1)}, u32[]{:S(2)}, u32[]{:S(2)}) collective-permute-start(bf16[4,3456]{1,0:T(4,128)(2,1)S(1)} %pad_maximum_fusion.1), channel_id=1, source_target_pairs={{0,16},{4,20},{8,24},{12,28},{16,0},{20,4},{24,8},{28,12},{1,17},{... | collective-permute-start | bytes 82952 | tf_op jit(solution)/shard_map/ppermute | solution.py:329
  46.8 2.0 %weight_terms.3 = bf16[176,1024]{1,0:T(8,128)(2,1)S(1)} custom-call(s32[4]{0:T(128)S(1)} %iota_xor_fusion.order, bf16[1,4,176,128]{3,2,1,0:T(8,128)(2,1)S(1)} %copy-done.12, bf16[2,4,176,128]{3,2,1,0:T(8,128)(2,1)S(1)} %get-tuple-element.36.refs_1_, bf16[1,4,176,128]{3,2,1,0:T(8,128)(2,1)S(1)} %get-tuple-element.37.refs_2_, ...), custom_call_target="tpu_custom_call" | custom-call | tf_op jit(solution)/shard_map/weight_terms/pallas_call | solution.py:133
  48.8 1.5 %collective-permute-start.11 = (bf16[176,1024]{1,0:T(8,128)(2,1)S(1)}, bf16[176,1024]{1,0:T(8,128)(2,1)S(1)}, u32[]{:S(2)}, u32[]{:S(2)}) collective-permute-start(bf16[176,1024]{1,0:T(8,128)(2,1)S(1)} %weight_terms.3), channel_id=1, source_target_pairs={{0,24},{4,28},{8,16},{12,20},{16,8},{20,12},{24,0},{28,4},{1,25},{... | collective-permute-start | bytes 1081352 | tf_op jit(solution)/shard_map/ppermute | solution.py:329
  50.4 2.8 %weight_terms.2 = (bf16[176,1024]{1,0:T(8,128)(2,1)S(1)}, bf16[176,1024]{1,0:T(8,128)(2,1)S(1)}, f32[176,1024]{1,0:T(8,128)S(1)}) custom-call(s32[4]{0:T(128)S(1)} %iota_xor_fusion.order, bf16[1,4,176,128]{3,2,1,0:T(8,128)(2,1)S(1)} %copy-done.12, bf16[2,4,176,128]{3,2,1,0:T(8,128)(2,1)S(1)} %get-tuple-element.36.refs_1_, ...), custom_call_target="tpu_custom_call" | custom-call | tf_op jit(solution)/shard_map/weight_terms/pallas_call | solution.py:133
  53.1 1.6 %collective-permute-start.12 = (bf16[176,1024]{1,0:T(8,128)(2,1)S(1)}, bf16[176,1024]{1,0:T(8,128)(2,1)S(1)}, u32[]{:S(2)}, u32[]{:S(2)}) collective-permute-start(bf16[176,1024]{1,0:T(8,128)(2,1)S(1)} %get-tuple-element.45), channel_id=1, source_target_pairs={{0,16},{4,20},{8,24},{12,28},{16,0},{20,4},{24,8},{28,12},{1,17},{... | collective-permute-start | bytes 1081352 | tf_op jit(solution)/shard_map/ppermute | solution.py:329
  55.2 0.8 %pad_maximum_fusion.refs_0_ = bf16[8,3456]{1,0:T(8,128)(2,1)S(1)} fusion(bf16[4,3456]{1,0:T(4,128)(2,1)S(1)} %collective-permute-done.16, bf16[2,3456]{1,0:T(2,128)(2,1)} %collective-permute-done.15, bf16[1,3456]{1,0:T(2,128)(2,1)} %collective-permute-done.14, bf16[1,3456]{1,0:T(2,128)(2,1)S(1)} %join_facts.1), kind=kLoop, calls=%fused_computation | loop fusion | flops 221184 | bytes 110592 | tf_op jit(solution)/shard_map/concatenate | solution.py:371
  56.0 0.9 %collective-permute-start.17 = (bf16[8,3456]{1,0:T(8,128)(2,1)S(1)}, bf16[8,3456]{1,0:T(8,128)(2,1)S(1)}, u32[]{:S(2)}, u32[]{:S(2)}) collective-permute-start(bf16[8,3456]{1,0:T(8,128)(2,1)S(1)} %pad_maximum_fusion.refs_0_), channel_id=1, source_target_pairs={{0,1},{1,0},{2,3},{3,2},{4,5},{5,4},{6,7},{7,6},{8,9},{9,8},{10,11... | collective-permute-start | bytes 165896 | tf_op jit(solution)/shard_map/ppermute | solution.py:329
  56.9 3.7 %collective-permute-done.17.refs_1_ = bf16[8,3456]{1,0:T(8,128)(2,1)S(1)} collective-permute-done((bf16[8,3456]{1,0:T(8,128)(2,1)S(1)}, bf16[8,3456]{1,0:T(8,128)(2,1)S(1)}, u32[]{:S(2)}, u32[]{:S(2)}) %collective-permute-start.17) | collective-permute-done | bytes 55328 | tf_op jit(solution)/shard_map/ppermute | solution.py:329
  60.6 2.4 %collective-permute-done.18.refs_2_ = bf16[8,3456]{1,0:T(8,128)(2,1)S(1)} collective-permute-done((bf16[8,3456]{1,0:T(8,128)(2,1)S(1)}, bf16[8,3456]{1,0:T(8,128)(2,1)S(1)}, u32[]{:S(2)}, u32[]{:S(2)}) %collective-permute-start.18) | collective-permute-done | bytes 55328 | tf_op jit(solution)/shard_map/ppermute | solution.py:329
  63.0 3.9 %collective-permute-done.19.refs_3_ = bf16[8,3456]{1,0:T(8,128)(2,1)S(1)} collective-permute-done((bf16[8,3456]{1,0:T(8,128)(2,1)S(1)}, bf16[8,3456]{1,0:T(8,128)(2,1)S(1)}, u32[]{:S(2)}, u32[]{:S(2)}) %collective-permute-start.19) | collective-permute-done | bytes 55328 | tf_op jit(solution)/shard_map/ppermute | solution.py:329
  67.7 3.4 %collective-permute-done.20.refs_2_ = f32[32,34]{1,0:T(8,128)S(1)} collective-permute-done((f32[32,34]{1,0:T(8,128)S(1)}, f32[32,34]{1,0:T(8,128)S(1)}, u32[]{:S(2)}, u32[]{:S(2)}) %collective-permute-start.20) | collective-permute-done | bytes 4384 | tf_op jit(solution)/shard_map/ppermute | solution.py:329
  72.5 4.1 %collective-permute-done.22.refs_4_ = f32[32,34]{1,0:T(8,128)S(1)} collective-permute-done((f32[32,34]{1,0:T(8,128)S(1)}, f32[32,34]{1,0:T(8,128)S(1)}, u32[]{:S(2)}, u32[]{:S(2)}) %collective-permute-start.22) | collective-permute-done | bytes 4384 | tf_op jit(solution)/shard_map/ppermute | solution.py:329
  76.7 0.9 %losses.1 = f32[2,4]{1,0:T(2,128)} custom-call(s32[1]{0:T(128)} %bitcast.9.place, f32[1]{0:T(128)S(6)} %copy.15.refs_0_, f32[32,34]{1,0:T(8,128)S(1)} %similarity_terms.1.refs_1_, f32[32,34]{1,0:T(8,128)S(1)} %collective-permute-done.20.refs_2_, f32[32,34]{1,0:T(8,128)S(1)} %collective-permute-done.21.refs_3_, f32[32,34]{1,0:T(8,128)S(1)} %collective-permute-done.22.refs_4_), custom_call_target="tpu_custom_call" | custom-call | tf_op jit(solution)/shard_map/losses/pallas_call | solution.py:313
  77.6 1.3 %arrange.1 = (bf16[4,32,512]{2,1,0:T(8,128)(2,1)}, bf16[4,32,512]{2,1,0:T(8,128)(2,1)}) custom-call(s32[4]{0:T(128)S(1)} %pad_add_fusion.place, bf16[1,32,512]{2,1,0:T(8,128)(2,1)S(1)} %get-tuple-element.27.refs_0_, bf16[1,32,512]{2,1,0:T(8,128)(2,1)S(1)} %copy-done.15, bf16[2,32,512]{2,1,0:T(8,128)(2,1)S(1)} %get-tuple-element.29.refs_2_, ...), custom_call_target="tpu_custom_call" | custom-call | tf_op jit(solution)/shard_map/arrange/pallas_call | solution.py:184
  78.9 0.9 %finish.1 = (f32[176,512]{1,0:T(8,128)}, f32[176,512]{1,0:T(8,128)}) custom-call(f32[176,1024]{1,0:T(8,128)S(1)} %get-tuple-element.44.refs_0_, bf16[176,1024]{1,0:T(8,128)(2,1)S(1)} %collective-permute-done.11.refs_1_, bf16[176,1024]{1,0:T(8,128)(2,1)S(1)} %collective-permute-done.12.refs_2_, bf16[176,1024]{1,0:T(8,128)(2,1)S(1)} %collective-permute-done.13.refs_3_), custom_call_target="tpu_custom_call" | custom-call | tf_op jit(solution)/shard_map/finish/pallas_call | solution.py:163
  (78 shorter events, 10.5 us)
Async XLA Ops:
  0.6 26.2 %collective-permute-start = (bf16[1,128,1408]{2,1,0:T(8,128)(2,1)}, bf16[1,128,1408]{2,1,0:T(8,128)(2,1)}, u32[]{:S(2)}, u32[]{:S(2)}) collective-permute-start(bf16[1,128,1408]{2,1,0:T(8,128)(2,1)} %refs_0_.2), channel_id=1, source_target_pairs={{0,1},{1,2},{2,3},{4,5},{5,6},{6,7},{8,9},{9,10},{10,11},{12,13},{... | collective-permute-start | bytes 1081352 | tf_op jit(solution)/shard_map/ppermute | solution.py:362
  6.3 21.9 %collective-permute-start.2 = (bf16[1,128,1408]{2,1,0:T(8,128)(2,1)}, bf16[1,128,1408]{2,1,0:T(8,128)(2,1)}, u32[]{:S(2)}, u32[]{:S(2)}) collective-permute-start(bf16[1,128,1408]{2,1,0:T(8,128)(2,1)} %refs_0_.2), channel_id=1, source_target_pairs={{3,2},{2,1},{1,0},{7,6},{6,5},{5,4},{11,10},{10,9},{9,8},{15,14},{... | collective-permute-start | bytes 1081352 | tf_op jit(solution)/shard_map/ppermute | solution.py:363
  7.6 26.0 %collective-permute-start.1 = (bf16[1,128,1408]{2,1,0:T(8,128)(2,1)}, bf16[1,128,1408]{2,1,0:T(8,128)(2,1)S(1)}, u32[]{:S(2)}, u32[]{:S(2)}) collective-permute-start(bf16[1,128,1408]{2,1,0:T(8,128)(2,1)} %refs_0_.2), channel_id=1, source_target_pairs={{0,3},{3,0},{4,7},{7,4},{8,11},{11,8},{12,15},{15,12},{16,19},{19,... | collective-permute-start | bytes 1081352 | tf_op jit(solution)/shard_map/ppermute | solution.py:366
  15.6 13.9 %collective-permute-start.14 = (bf16[1,3456]{1,0:T(2,128)(2,1)S(1)}, bf16[1,3456]{1,0:T(2,128)(2,1)}, u32[]{:S(2)}, u32[]{:S(2)}) collective-permute-start(bf16[1,3456]{1,0:T(2,128)(2,1)S(1)} %join_facts.1), channel_id=1, source_target_pairs={{0,4},{4,0},{8,12},{12,8},{16,20},{20,16},{24,28},{28,24},{1,5},{5... | collective-permute-start | bytes 20744 | tf_op jit(solution)/shard_map/ppermute | solution.py:329
  22.0 11.6 %copy-start.1 = (bf16[1408,512]{1,0:T(8,128)(2,1)S(1)}, bf16[1408,512]{1,0:T(8,128)(2,1)}, u32[]{:S(2)}) copy-start(bf16[1408,512]{1,0:T(8,128)(2,1)} %refs_2_.3) | copy-start | bytes 4325380
  22.0 11.6 %copy-start.3 = (bf16[1408,512]{1,0:T(8,128)(2,1)S(1)}, bf16[1408,512]{1,0:T(8,128)(2,1)}, u32[]{:S(2)}) copy-start(bf16[1408,512]{1,0:T(8,128)(2,1)} %refs_3_.3) | copy-start | bytes 4325380
  22.0 11.6 %copy-start.6 = (bf16[4,32,512]{2,1,0:T(8,128)(2,1)S(1)}, bf16[4,32,512]{2,1,0:T(8,128)(2,1)}, u32[]{:S(2)}) copy-start(bf16[4,32,512]{2,1,0:T(8,128)(2,1)} %refs_4_.6) | copy-start | bytes 393220
  22.0 11.7 %copy-start.8 = (bf16[4,32,512]{2,1,0:T(8,128)(2,1)S(1)}, bf16[4,32,512]{2,1,0:T(8,128)(2,1)}, u32[]{:S(2)}) copy-start(bf16[4,32,512]{2,1,0:T(8,128)(2,1)} %refs_5_.3) | copy-start | bytes 393220
  26.4 17.9 %collective-permute-start.5 = (bf16[1,4,176,128]{3,2,1,0:T(8,128)(2,1)}, bf16[1,4,176,128]{3,2,1,0:T(8,128)(2,1)}, u32[]{:S(2)}, u32[]{:S(2)}) collective-permute-start(bf16[1,4,176,128]{3,2,1,0:T(8,128)(2,1)} %get-tuple-element.38), channel_id=1, source_target_pairs={{0,4},{4,0},{8,12},{12,8},{16,20},{20,16},{24,28},{28,24},{1,5},{5... | collective-permute-start | bytes 540680 | tf_op jit(solution)/shard_map/ppermute | solution.py:329
  26.9 11.6 %collective-permute-start.3 = (bf16[1,128,1408]{2,1,0:T(8,128)(2,1)}, bf16[1,128,1408]{2,1,0:T(8,128)(2,1)}, u32[]{:S(2)}, u32[]{:S(2)}) collective-permute-start(bf16[1,128,1408]{2,1,0:T(8,128)(2,1)} %collective-permute-done.refs_0_), channel_id=1, source_target_pairs={{1,2},{2,3},{5,6},{6,7},{9,10},{10,11},{13,14},{14,15},{17,18},{18... | collective-permute-start | bytes 1081352 | tf_op jit(solution)/shard_map/ppermute | solution.py:362
  28.3 12.6 %collective-permute-start.4 = (bf16[1,128,1408]{2,1,0:T(8,128)(2,1)}, bf16[1,128,1408]{2,1,0:T(8,128)(2,1)}, u32[]{:S(2)}, u32[]{:S(2)}) collective-permute-start(bf16[1,128,1408]{2,1,0:T(8,128)(2,1)} %collective-permute-done.2.refs_3_), channel_id=1, source_target_pairs={{2,1},{1,0},{6,5},{5,4},{10,9},{9,8},{14,13},{13,12},{18,17},{17,1... | collective-permute-start | bytes 1081352 | tf_op jit(solution)/shard_map/ppermute | solution.py:363
  30.9 12.8 %collective-permute-start.15 = (bf16[2,3456]{1,0:T(2,128)(2,1)}, bf16[2,3456]{1,0:T(2,128)(2,1)}, u32[]{:S(2)}, u32[]{:S(2)}) collective-permute-start(bf16[2,3456]{1,0:T(2,128)(2,1)} %pad_maximum_fusion.2), channel_id=1, source_target_pairs={{0,8},{4,12},{8,0},{12,4},{16,24},{20,28},{24,16},{28,20},{1,9},{5... | collective-permute-start | bytes 41480 | tf_op jit(solution)/shard_map/ppermute | solution.py:329
  33.6 11.5 %collective-permute-start.8 = (bf16[128,1024]{1,0:T(8,128)(2,1)}, bf16[128,1024]{1,0:T(8,128)(2,1)S(1)}, u32[]{:S(2)}, u32[]{:S(2)}) collective-permute-start(bf16[128,1024]{1,0:T(8,128)(2,1)} %copy-done.9), channel_id=1, source_target_pairs={{0,4},{4,0},{8,12},{12,8},{16,20},{20,16},{24,28},{28,24},{1,5},{5... | collective-permute-start | bytes 786440 | tf_op jit(solution)/shard_map/ppermute | solution.py:329
  35.0 5.9 %copy-start.21 = (s32[3]{0:T(128)S(1)}, s32[3]{0:T(128)}, u32[]{:S(2)}) copy-start(s32[3]{0:T(128)} %add_add_fusion.1.flags) | copy-start | bytes 40
  38.4 8.3 %collective-permute-start.6 = (bf16[2,4,176,128]{3,2,1,0:T(8,128)(2,1)S(1)}, bf16[2,4,176,128]{3,2,1,0:T(8,128)(2,1)S(1)}, u32[]{:S(2)}, u32[]{:S(2)}) collective-permute-start(bf16[2,4,176,128]{3,2,1,0:T(8,128)(2,1)S(1)} %get-tuple-element.39), channel_id=1, source_target_pairs={{0,4},{4,0},{8,12},{12,8},{16,20},{20,16},{24,28},{28,24},{1,5},{5... | collective-permute-start | bytes 1081352 | tf_op jit(solution)/shard_map/ppermute | solution.py:329
  40.8 6.0 %copy-start.10 = (bf16[128,1024]{1,0:T(8,128)(2,1)S(1)}, bf16[128,1024]{1,0:T(8,128)(2,1)}, u32[]{:S(2)}) copy-start(bf16[128,1024]{1,0:T(8,128)(2,1)} %copy-done.9) | copy-start | bytes 786436
  40.8 6.0 %copy-start.12 = (bf16[1,4,176,128]{3,2,1,0:T(8,128)(2,1)S(1)}, bf16[1,4,176,128]{3,2,1,0:T(8,128)(2,1)}, u32[]{:S(2)}) copy-start(bf16[1,4,176,128]{3,2,1,0:T(8,128)(2,1)} %copy-done.11) | copy-start | bytes 540676
  40.8 5.9 %collective-permute-start.9 = (bf16[256,1024]{1,0:T(8,128)(2,1)S(1)}, bf16[256,1024]{1,0:T(8,128)(2,1)S(1)}, u32[]{:S(2)}, u32[]{:S(2)}) collective-permute-start(bf16[256,1024]{1,0:T(8,128)(2,1)S(1)} %get-tuple-element.42.refs_7_), channel_id=1, source_target_pairs={{0,4},{4,0},{8,12},{12,8},{16,20},{20,16},{24,28},{28,24},{1,5},{5... | collective-permute-start | bytes 1572872 | tf_op jit(solution)/shard_map/ppermute | solution.py:329
  43.7 3.0 %collective-permute-start.7 = (bf16[1,4,176,128]{3,2,1,0:T(8,128)(2,1)S(1)}, bf16[1,4,176,128]{3,2,1,0:T(8,128)(2,1)S(1)}, u32[]{:S(2)}, u32[]{:S(2)}) collective-permute-start(bf16[1,4,176,128]{3,2,1,0:T(8,128)(2,1)S(1)} %get-tuple-element.40), channel_id=1, source_target_pairs={{0,4},{4,0},{8,12},{12,8},{16,20},{20,16},{24,28},{28,24},{1,5},{5... | collective-permute-start | bytes 540680 | tf_op jit(solution)/shard_map/ppermute | solution.py:329
  44.3 2.5 %collective-permute-start.10 = (bf16[128,1024]{1,0:T(8,128)(2,1)S(1)}, bf16[128,1024]{1,0:T(8,128)(2,1)S(1)}, u32[]{:S(2)}, u32[]{:S(2)}) collective-permute-start(bf16[128,1024]{1,0:T(8,128)(2,1)S(1)} %get-tuple-element.43.refs_8_), channel_id=1, source_target_pairs={{0,4},{4,0},{8,12},{12,8},{16,20},{20,16},{24,28},{28,24},{1,5},{5... | collective-permute-start | bytes 786440 | tf_op jit(solution)/shard_map/ppermute | solution.py:329
  45.1 10.1 %collective-permute-start.16 = (bf16[4,3456]{1,0:T(4,128)(2,1)S(1)}, bf16[4,3456]{1,0:T(4,128)(2,1)S(1)}, u32[]{:S(2)}, u32[]{:S(2)}) collective-permute-start(bf16[4,3456]{1,0:T(4,128)(2,1)S(1)} %pad_maximum_fusion.1), channel_id=1, source_target_pairs={{0,16},{4,20},{8,24},{12,28},{16,0},{20,4},{24,8},{28,12},{1,17},{... | collective-permute-start | bytes 82952 | tf_op jit(solution)/shard_map/ppermute | solution.py:329
  48.8 18.1 %copy-start.4 = (bf16[1408,512]{1,0:T(8,128)(2,1)S(1)}, bf16[1408,512]{1,0:T(8,128)(2,1)}, u32[]{:S(2)}) copy-start(bf16[1408,512]{1,0:T(8,128)(2,1)} %refs_4_.7) | copy-start | bytes 4325380
  48.8 30.1 %collective-permute-start.11 = (bf16[176,1024]{1,0:T(8,128)(2,1)S(1)}, bf16[176,1024]{1,0:T(8,128)(2,1)S(1)}, u32[]{:S(2)}, u32[]{:S(2)}) collective-permute-start(bf16[176,1024]{1,0:T(8,128)(2,1)S(1)} %weight_terms.3), channel_id=1, source_target_pairs={{0,24},{4,28},{8,16},{12,20},{16,8},{20,12},{24,0},{28,4},{1,25},{... | collective-permute-start | bytes 1081352 | tf_op jit(solution)/shard_map/ppermute | solution.py:329
  53.1 24.5 %copy-start.15 = (bf16[1,32,512]{2,1,0:T(8,128)(2,1)S(1)}, bf16[1,32,512]{2,1,0:T(8,128)(2,1)}, u32[]{:S(2)}) copy-start(bf16[1,32,512]{2,1,0:T(8,128)(2,1)} %copy-done.14) | copy-start | bytes 98308
  53.1 25.7 %collective-permute-start.12 = (bf16[176,1024]{1,0:T(8,128)(2,1)S(1)}, bf16[176,1024]{1,0:T(8,128)(2,1)S(1)}, u32[]{:S(2)}, u32[]{:S(2)}) collective-permute-start(bf16[176,1024]{1,0:T(8,128)(2,1)S(1)} %get-tuple-element.45), channel_id=1, source_target_pairs={{0,16},{4,20},{8,24},{12,28},{16,0},{20,4},{24,8},{28,12},{1,17},{... | collective-permute-start | bytes 1081352 | tf_op jit(solution)/shard_map/ppermute | solution.py:329
  54.7 24.2 %collective-permute-start.13 = (bf16[176,1024]{1,0:T(8,128)(2,1)S(1)}, bf16[176,1024]{1,0:T(8,128)(2,1)S(1)}, u32[]{:S(2)}, u32[]{:S(2)}) collective-permute-start(bf16[176,1024]{1,0:T(8,128)(2,1)S(1)} %get-tuple-element.46), channel_id=1, source_target_pairs={{0,8},{4,12},{8,0},{12,4},{16,24},{20,28},{24,16},{28,20},{1,9},{5... | collective-permute-start | bytes 1081352 | tf_op jit(solution)/shard_map/ppermute | solution.py:329
  56.0 4.6 %collective-permute-start.17 = (bf16[8,3456]{1,0:T(8,128)(2,1)S(1)}, bf16[8,3456]{1,0:T(8,128)(2,1)S(1)}, u32[]{:S(2)}, u32[]{:S(2)}) collective-permute-start(bf16[8,3456]{1,0:T(8,128)(2,1)S(1)} %pad_maximum_fusion.refs_0_), channel_id=1, source_target_pairs={{0,1},{1,0},{2,3},{3,2},{4,5},{5,4},{6,7},{7,6},{8,9},{9,8},{10,11... | collective-permute-start | bytes 165896 | tf_op jit(solution)/shard_map/ppermute | solution.py:329
  56.9 6.1 %collective-permute-start.18 = (bf16[8,3456]{1,0:T(8,128)(2,1)S(1)}, bf16[8,3456]{1,0:T(8,128)(2,1)S(1)}, u32[]{:S(2)}, u32[]{:S(2)}) collective-permute-start(bf16[8,3456]{1,0:T(8,128)(2,1)S(1)} %pad_maximum_fusion.refs_0_), channel_id=1, source_target_pairs={{0,2},{1,3},{2,0},{3,1},{4,6},{5,7},{6,4},{7,5},{8,10},{9,11},{10,... | collective-permute-start | bytes 165896 | tf_op jit(solution)/shard_map/ppermute | solution.py:329
  60.6 6.2 %collective-permute-start.19 = (bf16[8,3456]{1,0:T(8,128)(2,1)S(1)}, bf16[8,3456]{1,0:T(8,128)(2,1)S(1)}, u32[]{:S(2)}, u32[]{:S(2)}) collective-permute-start(bf16[8,3456]{1,0:T(8,128)(2,1)S(1)} %pad_maximum_fusion.refs_0_), channel_id=1, source_target_pairs={{0,3},{1,2},{2,1},{3,0},{4,7},{5,6},{6,5},{7,4},{8,11},{9,10},{10,... | collective-permute-start | bytes 165896 | tf_op jit(solution)/shard_map/ppermute | solution.py:329
  67.3 3.8 %collective-permute-start.20 = (f32[32,34]{1,0:T(8,128)S(1)}, f32[32,34]{1,0:T(8,128)S(1)}, u32[]{:S(2)}, u32[]{:S(2)}) collective-permute-start(f32[32,34]{1,0:T(8,128)S(1)} %similarity_terms.1.refs_1_), channel_id=1, source_target_pairs={{0,1},{1,0},{2,3},{3,2},{4,5},{5,4},{6,7},{7,6},{8,9},{9,8},{10,11... | collective-permute-start | bytes 13064 | tf_op jit(solution)/shard_map/ppermute | solution.py:329
  67.4 5.1 %collective-permute-start.21 = (f32[32,34]{1,0:T(8,128)S(1)}, f32[32,34]{1,0:T(8,128)S(1)}, u32[]{:S(2)}, u32[]{:S(2)}) collective-permute-start(f32[32,34]{1,0:T(8,128)S(1)} %similarity_terms.1.refs_1_), channel_id=1, source_target_pairs={{0,2},{1,3},{2,0},{3,1},{4,6},{5,7},{6,4},{7,5},{8,10},{9,11},{10,... | collective-permute-start | bytes 13064 | tf_op jit(solution)/shard_map/ppermute | solution.py:329
  71.2 5.5 %collective-permute-start.22 = (f32[32,34]{1,0:T(8,128)S(1)}, f32[32,34]{1,0:T(8,128)S(1)}, u32[]{:S(2)}, u32[]{:S(2)}) collective-permute-start(f32[32,34]{1,0:T(8,128)S(1)} %similarity_terms.1.refs_1_), channel_id=1, source_target_pairs={{0,3},{1,2},{2,1},{3,0},{4,7},{5,6},{6,5},{7,4},{8,11},{9,10},{10,... | collective-permute-start | bytes 13064 | tf_op jit(solution)/shard_map/ppermute | solution.py:329
  (14 other events, 16.7 us)
where the time goes:
time: 80.5 us; the launch traced here: 79.8 us
  starting transfers between devices  26.6 us (33%)
  waiting for transfers between devices  19.4 us (24%)
  Pallas kernels  17 us (21%)
  local copies, waits for them, and re-layouts  11.5 us (14%)
  other arithmetic  3.67 us (5%)
  between operations  1.58 us (2%)
    ppermute x18, waiting for transfers between devices, flip(): return lax.ppermute(array, axis, [(n, n ^ mask) for n in range(count)])  17.5 us
    unnamed x46, local copies, waits for them, and re-layouts  10.8 us
    ppermute x18, starting transfers between devices, flip(): return lax.ppermute(array, axis, [(n, n ^ mask) for n in range(count)])  10.4 us
    pallas_call x3, Pallas kernels, image_group(): pl.pallas_call(functools.partial(group_kernel, width // HD, [len(c) for c...  8.72 us
    ppermute x2, starting transfers between devices, work(): right[d] = lax.ppermute(right[d - 1], 'mp', ups)  7.08 us
    ppermute x1, starting transfers between devices, work(): right[n_mp - 1] = left[n_mp - 1] = lax.ppermute(img_tokens, 'mp', ends)  6.62 us
    pallas_call x2, Pallas kernels, weight_terms(): pl.pallas_call(functools.partial(terms_kernel, count, pieces), grid_spec=...  4.76 us
    concatenate x3, other arithmetic, work(): facts = jnp.concatenate([facts, flip(facts, 'dp', n_dp, mask)], axis=0)  2.93 us
  transfers between devices with their start and end apart: 23, of which 6 were waited for; matrix products, arithmetic and copies ran while one was open for 5% of the time, Pallas kernels for 20%

commit v1 on v0

--- a/solution.py
+++ b/solution.py
@@ -17,32 +17,36 @@
     return lax.dot_general(a, b, (((ca,), (cb,)), ((), ())), preferred_element_type=F32)
 
 
-def pick(ready, choices, store):
+def room(*arrays):
+    total = sum(a.size * a.dtype.itemsize for a in arrays)
+    return pltpu.CompilerParams(vmem_limit_bytes=min(2 * total + 3 * 2**20, 60 * 2**20))
+
+
+def pick(flag, choices, store):
     if len(choices) == 1:
         store[...] = choices[0][0]
         return
-
-    @pl.when(ready == 1)
-    def _():
-        store[...] = choices[0][0]
-
-    @pl.when(ready == 0)
-    def _():
-        store[...] = choices[1][0]
-
-
-def group_kernel(heads, counts, flags, lens, *refs):
+    for number, choice in enumerate(choices):
+
+        @pl.when(flag == number)
+        def _(choice=choice):
+            store[...] = choice[0]
+
+
+def group_kernel(heads, counts, rules, ids, lens, *refs):
     n = len(counts)
-    inputs, rest = refs[: sum(counts)], refs[sum(counts) :]
+    which = [rule[0](ids[1]) for rule in rules]
+    image = [rule[1](ids[1]) for rule in rules]
+    inputs, rest = refs[: sum(counts)], refs[sum(counts) + 1 :]
     wk, wv, qs, dos, att, gq, grads, kept, sent, store, turned = rest
     inv = HD ** (-0.5)
     width = heads * HD
     image_len = store.shape[0] // n
-    core = flags[2 * n]
+    core = ids[0] & 1
     spans = [slice(s * image_len, (s + 1) * image_len) for s in range(n)]
     at = 0
     for s, count in enumerate(counts):
-        pick(flags[s], inputs[at : at + count], store.at[spans[s]])
+        pick(which[s], inputs[at : at + count], store.at[spans[s]])
         at += count
     x = store[...]
     keys = jnp.dot(x, wk[...], preferred_element_type=F32).astype(BF16)
@@ -59,13 +63,13 @@
     pairs = [(s, c) for s in range(n) for c in cols]
     keep = []
     for s in range(n):
-        length = lens[flags[n + s]]
+        length = lens[image[s]]
         at_row = lax.broadcasted_iota(jnp.int32, (qs.shape[1], HD), 0)
         keep.append((at_row < length).astype(F32))
     k = [keys[spans[s], c] for s, c in pairs]
     v = [values[spans[s], c] for s, c in pairs]
-    q = [qs[flags[n + s], :, c] for s, c in pairs]
-    masked = [(dos[flags[n + s], :, c].astype(F32) * keep[s]).astype(BF16) for s, c in pairs]
+    q = [qs[image[s], :, c] for s, c in pairs]
+    masked = [(dos[image[s], :, c].astype(F32) * keep[s]).astype(BF16) for s, c in pairs]
     scores = [dot(a, b, 1, 1) * inv for a, b in zip(q, k)]
     grad_probs = [dot(a, b, 1, 1) for a, b in zip(masked, v)]
     tops = [jnp.max(s, axis=1, keepdims=True) for s in scores]
@@ -84,7 +88,8 @@
         gq[s, :, c] = dot(grad_scores[i], k[i], 1, 0).astype(BF16)
 
 
-def image_group(flags, lengths, choices, n_dp, w_key, w_value, queries, d_out):
+def image_group(ids, lengths, members, n_dp, w_key, w_value, queries, d_out, first):
+    choices, rules = [m[0] for m in members], [m[1:] for m in members]
     n = len(choices)
     caption_len, width = queries.shape[1:]
     image_len, feats = choices[0][0].shape[1:]
@@ -98,52 +103,84 @@
         (n, half, rows, image_len),
     ]
     full = lambda shape: pl.BlockSpec(shape, lambda i, a, b: (0,) * len(shape))
-    operands = [*flat, w_key, w_value, queries, d_out]
-    return pl.pallas_call(
-        functools.partial(group_kernel, width // HD, [len(c) for c in choices]),
+    operands = [*flat, first, w_key, w_value, queries, d_out]
+    results = [jax.ShapeDtypeStruct(s, BF16) for s in shapes]
+    return pl.pallas_call(
+        functools.partial(group_kernel, width // HD, [len(c) for c in choices], rules),
         grid_spec=pltpu.PrefetchScalarGridSpec(
             num_scalar_prefetch=2,
             grid=(1,),
-            in_specs=[full(o.shape) for o in operands],
+            in_specs=[full(o.shape) for o in flat]
+            + [pl.BlockSpec(memory_space=pl.ANY)]
+            + [full(o.shape) for o in operands[-4:]],
             out_specs=[full(s) for s in shapes],
             scratch_shapes=[
                 pltpu.VMEM((n * image_len, feats), BF16),
                 pltpu.VMEM((n_dp, rows, image_len), BF16),
             ],
         ),
-        out_shape=[jax.ShapeDtypeStruct(s, BF16) for s in shapes],
-        compiler_params=pltpu.CompilerParams(vmem_limit_bytes=20 * 2**20),
+        out_shape=results,
+        compiler_params=room(*operands, *results, operands[0]),
         name="image_group",
-    )(flags, lengths, *operands)
-
-
-def terms_kernel(count, pieces, order, *refs):
-    turned, grads, outs = refs[:count], refs[count : 2 * count], refs[2 * count :]
-    right = jnp.concatenate([g[...] for g in grads], axis=0)
-    for piece, out in zip(pieces, outs):
-        place = order[piece]
-        left = jnp.concatenate([t[s, place] for t in turned for s in range(t.shape[0])], axis=1)
-        out[...] = jnp.dot(left, right, preferred_element_type=F32).astype(out.dtype)
-
-
-def weight_terms(order, pieces, turned, grads):
+    )(ids, lengths, *operands)
+
+
+def joined(turned, grads, place):
+    left = jnp.concatenate([t[s, place] for t in turned for s in range(t.shape[0])], axis=1)
+    return jnp.dot(left, jnp.concatenate([g[...] for g in grads]), preferred_element_type=F32)
+
+
+def early_kernel(count, *refs):
+    turned, grads, out = refs[:count], refs[count : 2 * count], refs[2 * count]
+    for place in range(out.shape[0]):
+        out[place] = joined(turned, grads, place)
+
+
+def early_terms(turned, grads):
+    half, rows = turned[0].shape[1:3]
+    result = jax.ShapeDtypeStruct((half, rows, grads[0].shape[1]), F32)
+    return pl.pallas_call(
+        functools.partial(early_kernel, len(turned)),
+        out_shape=result,
+        compiler_params=room(*turned, *grads, result),
+        name="early_terms",
+    )(*turned, *grads)
+
+
+def terms_kernel(count, pieces, ids, *refs):
+    turned, grads, early = refs[:count], refs[count : 2 * count], refs[2 * count]
+    for piece, out in zip(pieces, refs[2 * count + 1 :]):
+        place = (ids[0] >> 1) ^ piece
+        out[...] = (early[place] + joined(turned, grads, place)).astype(out.dtype)
+
+
+def weight_terms(ids, pieces, turned, grads, early):
     count = len(turned)
-    rows, width = turned[0].shape[2], grads[0].shape[1]
+    rows, width = early.shape[1:]
     full = lambda shape: pl.BlockSpec(shape, lambda i, o: (0,) * len(shape))
-    return pl.pallas_call(
-        functools.partial(terms_kernel, count, pieces),
+    one = pl.BlockSpec((1, rows, width), lambda i, o: ((o[0] >> 1) ^ pieces[0], 0, 0))
+    results = [jax.ShapeDtypeStruct((rows, width), F32 if p == 0 else BF16) for p in pieces]
+    if len(pieces) == 1:
+        kernel = functools.partial(one_kernel, count, pieces[0])
+    else:
+        one, kernel = full(early.shape), functools.partial(terms_kernel, count, pieces)
+    return pl.pallas_call(
+        kernel,
         grid_spec=pltpu.PrefetchScalarGridSpec(
             num_scalar_prefetch=1,
             grid=(1,),
-            in_specs=[full(o.shape) for o in (*turned, *grads)],
+            in_specs=[full(o.shape) for o in (*turned, *grads)] + [one],
             out_specs=[full((rows, width))] * len(pieces),
         ),
-        out_shape=[
-            jax.ShapeDtypeStruct((rows, width), F32 if piece == 0 else BF16) for piece in pieces
-        ],
-        compiler_params=pltpu.CompilerParams(vmem_limit_bytes=20 * 2**20),
+        out_shape=results,
+        compiler_params=room(*turned, *grads, *results, early),
         name="weight_terms",
-    )(order, *turned, *grads)
+    )(ids, *turned, *grads, early)
+
+
+def one_kernel(count, piece, ids, *refs):
+    turned, grads, early, out = refs[:count], refs[count : 2 * count], *refs[2 * count :]
+    out[...] = (early[0] + joined(turned, grads, (ids[0] >> 1) ^ piece)).astype(out.dtype)
 
 
 def finish_kernel(*refs):
@@ -163,26 +200,26 @@
     return pl.pallas_call(
         finish_kernel,
         out_shape=[shape, shape],
-        compiler_params=pltpu.CompilerParams(vmem_limit_bytes=12 * 2**20),
+        compiler_params=room(own, own, *arrived),
         name="finish",
     )(own, *arrived)
 
 
-def arrange_kernel(slots, place, *refs):
+def arrange_kernel(slots, rules, ids, *refs):
     count = len(slots)
     at = 0
     for g, several in enumerate(slots):
         for s in range(several):
             for side in range(2):
-                refs[2 * count + side][place[at]] = refs[2 * g + side][s]
+                refs[2 * count + side][rules[at](ids[1])] = refs[2 * g + side][s]
             at += 1
 
 
-def arrange(images, parts, slots):
+def arrange(ids, rules, parts, slots):
     shape = (sum(slots), *parts[0].shape[1:])
     full = lambda shape: pl.BlockSpec(shape, lambda i, o: (0,) * len(shape))
     return pl.pallas_call(
-        functools.partial(arrange_kernel, slots),
+        functools.partial(arrange_kernel, slots, rules),
         grid_spec=pltpu.PrefetchScalarGridSpec(
             num_scalar_prefetch=1,
             grid=(1,),
@@ -190,9 +227,9 @@
             out_specs=[full(shape)] * 2,
         ),
         out_shape=[jax.ShapeDtypeStruct(shape, BF16)] * 2,
-        compiler_params=pltpu.CompilerParams(vmem_limit_bytes=12 * 2**20),
+        compiler_params=room(*parts, *parts),
         name="arrange",
-    )(images, *parts)
+    )(ids, *parts)
 
 
 def facts_kernel(pooled, texts, out):
@@ -202,6 +239,47 @@
         out[:, feats + c * width : feats + (c + 1) * width] = texts[c : c + 1, :]
 
 
+def tick_kernel(ids, out):
+    out[...] = jnp.zeros_like(out) + ids[0]
+
+
+def tick(ids):
+    return pl.pallas_call(
+        tick_kernel,
+        grid_spec=pltpu.PrefetchScalarGridSpec(
+            num_scalar_prefetch=1,
+            grid=(1,),
+            in_specs=[],
+            out_specs=pl.BlockSpec((8, HD), lambda i, o: (0, 0)),
+        ),
+        out_shape=jax.ShapeDtypeStruct((8, HD), jnp.int32),
+        cost_estimate=pl.CostEstimate(flops=10**9, bytes_accessed=24 * 2**20, transcendentals=0),
+        compiler_params=pltpu.CompilerParams(vmem_limit_bytes=2**20),
+        name="tick",
+    )(ids)
+
+
+def append_kernel(first, second, out, *pooled):
+    rows = first.shape[0]
+    out[:rows] = first[...]
+    out[rows:] = second[...]
+    for part in pooled:
+        feats = part.shape[1]
+        part[:rows] = first[:, :feats]
+        part[rows:] = second[:, :feats]
+
+
+def append(first, second, feats):
+    rows, width = first.shape
+    shapes = [(2 * rows, width)] + ([(2 * rows, feats)] if feats else [])
+    return pl.pallas_call(
+        append_kernel,
+        out_shape=[jax.ShapeDtypeStruct(s, first.dtype) for s in shapes],
+        compiler_params=room(first, second, first, second, first, second),
+        name="append",
+    )(first, second)
+
+
 def join_facts(pooled, texts):
     return pl.pallas_call(
         facts_kernel,
@@ -211,13 +289,13 @@
     )(pooled, texts)
 
 
-def sims_kernel(place, *refs):
+def sims_kernel(ids, *refs):
     facts, (w_proj, out, rows, texts) = refs[:-4], refs[-4:]
     n_dp = facts[0].shape[0]
     feats, width = w_proj.shape
     captions = texts.shape[0] // n_dp
     for r, piece in enumerate(facts):
-        start = pl.multiple_of((place[0] ^ r) * n_dp, n_dp)
+        start = pl.multiple_of((ids[1] ^ r) * n_dp, n_dp)
         rows[pl.ds(start, n_dp)] = piece[:, :feats].astype(F32)
     for c in range(captions):
         texts[c * n_dp : (c + 1) * n_dp] = facts[0][
@@ -234,7 +312,7 @@
     out[:, count + 1 : count + 2] = jnp.sum(txt * txt, axis=1, keepdims=True)
 
 
-def similarity_terms(place, facts, w_proj, captions):
+def similarity_terms(ids, facts, w_proj, captions):
     n_dp = facts[0].shape[0]
     count, feats = n_dp * len(facts), w_proj.shape[0]
     full = lambda shape: pl.BlockSpec(shape, lambda i, o: (0,) * len(shape))
@@ -251,15 +329,15 @@
             ],
         ),
         out_shape=jax.ShapeDtypeStruct((count, n_dp * captions + 2), F32),
-        compiler_params=pltpu.CompilerParams(vmem_limit_bytes=16 * 2**20),
+        compiler_params=room(*facts, w_proj, facts[0], facts[0], facts[0]),
         name="similarity_terms",
-    )(place, *facts, w_proj)
-
-
-def losses_kernel(n_dp, place, *refs):
+    )(ids, *facts, w_proj)
+
+
+def losses_kernel(n_dp, ids, *refs):
     inv_temp, terms, (out, store) = refs[0], refs[1:-2], refs[-2:]
     for r, term in enumerate(terms):
-        store[place[0] ^ r] = term[...]
+        store[ids[1] ^ r] = term[...]
     total = store[0]
     for r in range(1, len(terms)):
         total = total + store[r]
@@ -286,12 +364,12 @@
     out[1:2, :] = caption_side[:, :captions]
 
 
-def large_losses(place, inv_temp, terms, n_dp):
+def large_losses(ids, inv_temp, terms, n_dp):
     count = terms[0].shape[0]
     stacked = jnp.stack(terms)
-    total = stacked[place[0] ^ 0]
+    total = stacked[ids[1]]
     for z in range(1, len(terms)):
-        total = total + stacked[place[0] ^ z]
+        total = total + stacked[ids[1] ^ z]
     img_sq, txt_sq = total[:, count], total[:, count + 1]
     logits = (
         inv_temp[0]
@@ -305,10 +383,10 @@
     return jnp.stack([image_side, caption_side])
 
 
-def losses(place, inv_temp, terms, n_dp, captions):
+def losses(ids, inv_temp, terms, n_dp, captions):
     shape = terms[0].shape
     if shape[0] > HD:
-        return large_losses(place, inv_temp, terms, n_dp)
+        return large_losses(ids, inv_temp, terms, n_dp)
     full = lambda shape: pl.BlockSpec(shape, lambda i, o: (0,) * len(shape))
     return pl.pallas_call(
         functools.partial(losses_kernel, n_dp),
@@ -320,9 +398,9 @@
             scratch_shapes=[pltpu.VMEM((len(terms), *shape), F32)],
         ),
         out_shape=jax.ShapeDtypeStruct((2, captions), F32),
-        compiler_params=pltpu.CompilerParams(vmem_limit_bytes=40 * 2**20),
+        compiler_params=room(*terms),
         name="losses",
-    )(place, inv_temp, *terms)
+    )(ids, inv_temp, *terms)
 
 
 def flip(array, axis, count, mask):
@@ -333,8 +411,30 @@
     return work(n_dp, n_mp, *args)
 
 
-def slot_groups(n_mp):
-    return [[0], [1, n_mp - 1]] + [[s] for s in range(n_mp - 2, 1, -1)]
+def gather_images(tokens, n_mp):
+    first = lambda z: 0
+    own = ([tokens], first, lambda z: z)
+    if n_mp != 4:
+        rest = []
+        for s in range(1, n_mp):
+            pairs = [(n, (n + s) % n_mp) for n in range(n_mp)]
+            rule = lambda z, s=s: lax.rem(z + (n_mp - s), n_mp)
+            rest.append([([lax.ppermute(tokens, "mp", pairs)], first, rule)])
+        return [[own], *rest]
+    right = lax.ppermute(tokens, "mp", [(0, 1), (1, 2), (2, 3)])
+    left = lax.ppermute(tokens, "mp", [(1, 0), (2, 1), (3, 2)])
+    far = lax.ppermute(tokens, "mp", [(0, 3), (3, 0)])
+    right_on = lax.ppermute(right, "mp", [(1, 2), (2, 3)])
+    left_on = lax.ppermute(left, "mp", [(1, 0), (2, 1)])
+    inner = lambda z: (z == 1) | (z == 2)
+    near = ([left, right], lambda z: z & 1, lambda z: z ^ 1)
+    other = (
+        [far, left, right],
+        lambda z: jnp.where(inner(z), z, 0),
+        lambda z: z ^ 3,
+    )
+    last = ([left_on, right_on], lambda z: z >> 1, lambda z: z ^ 2)
+    return [[own], [near], [other], [last]]
 
 
 def work(
@@ -351,36 +451,24 @@
     txt_embed,
     inv_temp,
 ):
-    group = lax.axis_index("dp").astype(jnp.int32)
-    place = lax.axis_index("mp").astype(jnp.int32)
+    ids = jnp.stack([lax.axis_index("dp"), lax.axis_index("mp")]).astype(jnp.int32)
     captions = queries.shape[0]
 
-    right, left = {0: img_tokens}, {0: img_tokens}
-    for d in range(1, n_mp - 1):
-        ups = [(n, n + 1) for n in range(d - 1, n_mp - 1)]
-        downs = [(n_mp - 1 - a, n_mp - 1 - b) for a, b in ups]
-        right[d] = lax.ppermute(right[d - 1], "mp", ups)
-        left[d] = lax.ppermute(left[d - 1], "mp", downs)
-        if d == 1:
-            ends = [(0, n_mp - 1), (n_mp - 1, 0)]
-            right[n_mp - 1] = left[n_mp - 1] = lax.ppermute(img_tokens, "mp", ends)
+    groups = gather_images(img_tokens, n_mp)
+    feats = img_pooled.shape[1]
 
     facts = join_facts(img_pooled, txt_embed)
     mask = 1
     while mask < n_dp:
-        facts = jnp.concatenate([facts, flip(facts, "dp", n_dp, mask)], axis=0)
+        got = flip(facts, "dp", n_dp, mask)
+        facts, *pooled = append(facts, got, feats if 2 * mask == n_dp else 0)
         mask *= 2
 
-    core = group % 2
-    parts, turned, others, grads, other_grads, images = [], [], [], [], [], []
-    groups = slot_groups(n_mp)
-    for slots in groups:
-        choices = [[right[s], left[n_mp - s]] if s else [img_tokens] for s in slots]
-        here = [(place - s) % n_mp for s in slots]
-        images += here
-        flags = jnp.stack([(place >= s).astype(jnp.int32) for s in slots] + here + [core])
+    first = tick(ids)
+    parts, turned, others, grads, other_grads = [], [], [], [], []
+    for members in groups:
         att, gq, grad, kept, sent = image_group(
-            flags, lengths, choices, n_dp, w_key, w_value, queries, d_out
+            ids, lengths, members, n_dp, w_key, w_value, queries, d_out, first
         )
         parts += [att, gq]
         turned.append(kept)
@@ -389,21 +477,22 @@
         other_grads.append(flip(grad, "dp", n_dp, 1))
 
     half = n_dp // 2
-    order = ((group // 2) ^ jnp.arange(half)).astype(jnp.int32)
-    sides = (turned + others, grads + other_grads)
-    (last,) = weight_terms(order, (half - 1,), *sides)
+    early = early_terms(turned[:-1] + others[:-1], grads[:-1] + other_grads[:-1])
+    sides = (turned[-1:] + others[-1:], grads[-1:] + other_grads[-1:], early)
+    (last,) = weight_terms(ids, (half - 1,), *sides)
     arrived = [flip(last, "dp", n_dp, 2 * (half - 1))]
-    pieces = weight_terms(order, tuple(range(half - 2, -1, -1)), *sides)
+    pieces = weight_terms(ids, tuple(range(half - 2, -1, -1)), *sides)
     for m, piece in zip(range(half - 2, 0, -1), pieces):
         arrived.append(flip(piece, "dp", n_dp, 2 * m))
-    attended, grad_queries = arrange(jnp.stack(images), parts, [len(s) for s in groups])
+    rules = [m[2] for members in groups for m in members]
+    attended, grad_queries = arrange(ids, rules, parts, [len(m) for m in groups])
     dw_key, dw_value = finish(pieces[-1], arrived)
 
-    pools = [facts] + [flip(facts, "mp", n_mp, m) for m in range(1, n_mp)]
-    spot = place.reshape(1)
-    terms = similarity_terms(spot, pools, w_proj, captions)
+    (pooled,) = pooled
+    pools = [facts] + [flip(pooled, "mp", n_mp, m) for m in range(1, n_mp)]
+    terms = similarity_terms(ids, pools, w_proj, captions)
     terms = [terms] + [flip(terms, "mp", n_mp, m) for m in range(1, n_mp)]
-    contrast = losses(spot, inv_temp, terms, n_dp, captions)
+    contrast = losses(ids, inv_temp, terms, n_dp, captions)
     return (attended, grad_queries, dw_key, dw_value, contrast)
 
 

time: 80.5 us -> 89.7 us (1.11)
  waiting for transfers between devices: 19.4 us -> 34.8 us
  local copies, waits for them, and re-layouts: 11.5 us -> 1.38 us
  starting transfers between devices: 26.6 us -> 36.1 us
  other arithmetic: 3.67 us -> 0.08 us
  Pallas kernels: 17 us -> 15.7 us
    ppermute x18 -> x20, starting transfers between devices: 10.4 us -> 23.4 us  [flip(): return lax.ppermute(array, axis, [(n, n ^ mask) for n in range(count)])]
    unnamed x46 -> x18, local copies, waits for them, and re-layouts: 10.8 us -> 1.38 us
    ppermute x5, waiting for transfers between devices: 1.83 us -> 10.4 us  [the longest x1 3.88 us: gather_images(): left_on = lax.ppermute(left, 'mp', [(1, 0), (2, 1)])]
    ppermute x18 -> x20, waiting for transfers between devices: 17.5 us -> 24.3 us  [flip(): return lax.ppermute(array, axis, [(n, n ^ mask) for n in range(count)])]
    ppermute x5, starting transfers between devices: 16.3 us -> 12.6 us  [the longest x1 5.61 us: gather_images(): right = lax.ppermute(tokens, 'mp', [(0, 1), (1, 2), (2, 3)])]
    concatenate x3 -> x0, other arithmetic: 2.93 us -> none  [work(): facts = jnp.concatenate([facts, flip(facts, 'dp', n_dp, mask)], axis=0)]
    pallas_call x3 -> x4, Pallas kernels: 8.72 us -> 7.28 us  [image_group(): pl.pallas_call(functools.partial(group_kernel, width // HD, [len(c) for c...]
    pallas_call x4 -> x9, Pallas kernels: 6.95 us -> 5.94 us  [the longest x2 1.8 us: weight_terms(): pl.pallas_call(kernel, grid_spec=pltpu.PrefetchScalarGridSpec(num_scalar_...]
  transfers between devices with their start and end apart: 23 -> 25, of which waited for: 6 -> 13; matrix products, arithmetic and copies ran while one was open for 5% -> 0% of each run, Pallas kernels for 20% -> 16%
where the time goes in v1:
time: 89.7 us; the launch traced here: 89.5 us
  starting transfers between devices  36.1 us (40%)
  waiting for transfers between devices  34.8 us (39%)
  Pallas kernels  15.7 us (18%)
  between operations  1.52 us (2%)
  local copies, waits for them, and re-layouts  1.38 us (2%)
    ppermute x20, waiting for transfers between devices, flip(): return lax.ppermute(array, axis, [(n, n ^ mask) for n in range(count)])  24.3 us
    ppermute x20, starting transfers between devices, flip(): return lax.ppermute(array, axis, [(n, n ^ mask) for n in range(count)])  23.4 us
    pallas_call x4, Pallas kernels, image_group(): pl.pallas_call(functools.partial(group_kernel, width // HD, [len(c) for c...  7.28 us
    ppermute x1, starting transfers between devices, gather_images(): right = lax.ppermute(tokens, 'mp', [(0, 1), (1, 2), (2, 3)])  5.61 us
    ppermute x1, waiting for transfers between devices, gather_images(): left_on = lax.ppermute(left, 'mp', [(1, 0), (2, 1)])  3.88 us
    ppermute x1, starting transfers between devices, gather_images(): far = lax.ppermute(tokens, 'mp', [(0, 3), (3, 0)])  3.75 us
    ppermute x1, waiting for transfers between devices, gather_images(): left = lax.ppermute(tokens, 'mp', [(1, 0), (2, 1), (3, 2)])  2.89 us
    ppermute x1, waiting for transfers between devices, gather_images(): far = lax.ppermute(tokens, 'mp', [(0, 3), (3, 0)])  2.54 us
  transfers between devices with their start and end apart: 25, of which 13 were waited for; matrix products, arithmetic and copies ran while one was open for 0% of the time, Pallas kernels for 16%

profile of v1, /device:TPU:0, one launch (start us, length us, event | category | flops | bytes accessed | tf_op | source)
XLA Modules:
  0.0 89.5 jit_solution(7843729235102537833)
XLA Ops:
  0.6 1.3 %collective-permute-start = (bf16[1,128,1408]{2,1,0:T(8,128)(2,1)}, bf16[1,128,1408]{2,1,0:T(8,128)(2,1)S(1)}, u32[]{:S(2)}, u32[]{:S(2)}) collective-permute-start(bf16[1,128,1408]{2,1,0:T(8,128)(2,1)} %refs_0_.2), channel_id=1, source_target_pairs={{1,0},{2,1},{3,2},{5,4},{6,5},{7,6},{9,8},{10,9},{11,10},{13,12},{... | collective-permute-start | bytes 1081352 | tf_op jit(solution)/shard_map/ppermute | solution.py:425
  1.9 5.6 %collective-permute-start.1 = (bf16[1,128,1408]{2,1,0:T(8,128)(2,1)}, bf16[1,128,1408]{2,1,0:T(8,128)(2,1)S(1)}, u32[]{:S(2)}, u32[]{:S(2)}) collective-permute-start(bf16[1,128,1408]{2,1,0:T(8,128)(2,1)} %refs_0_.2), channel_id=1, source_target_pairs={{0,1},{1,2},{2,3},{4,5},{5,6},{6,7},{8,9},{9,10},{10,11},{12,13},{... | collective-permute-start | bytes 1081352 | tf_op jit(solution)/shard_map/ppermute | solution.py:424
  7.5 3.8 %collective-permute-start.2 = (bf16[1,128,1408]{2,1,0:T(8,128)(2,1)}, bf16[1,128,1408]{2,1,0:T(8,128)(2,1)S(1)}, u32[]{:S(2)}, u32[]{:S(2)}) collective-permute-start(bf16[1,128,1408]{2,1,0:T(8,128)(2,1)} %refs_0_.2), channel_id=1, source_target_pairs={{0,3},{3,0},{4,7},{7,4},{8,11},{11,8},{12,15},{15,12},{16,19},{19,... | collective-permute-start | bytes 1081352 | tf_op jit(solution)/shard_map/ppermute | solution.py:426
  11.3 2.9 %collective-permute-done.refs_0_.refs_1_ = bf16[1,128,1408]{2,1,0:T(8,128)(2,1)S(1)} collective-permute-done((bf16[1,128,1408]{2,1,0:T(8,128)(2,1)}, bf16[1,128,1408]{2,1,0:T(8,128)(2,1)S(1)}, u32[]{:S(2)}, u32[]{:S(2)}) %collective-permute-start) | collective-permute-done | bytes 360480 | tf_op jit(solution)/shard_map/ppermute | solution.py:425
  14.2 1.3 %collective-permute-start.3 = (bf16[1,128,1408]{2,1,0:T(8,128)(2,1)S(1)}, bf16[1,128,1408]{2,1,0:T(8,128)(2,1)S(1)}, u32[]{:S(2)}, u32[]{:S(2)}) collective-permute-start(bf16[1,128,1408]{2,1,0:T(8,128)(2,1)S(1)} %collective-permute-done.refs_0_.refs_1_), channel_id=1, source_target_pairs={{1,0},{2,1},{5,4},{6,5},{9,8},{10,9},{13,12},{14,13},{17,16},{18,1... | collective-permute-start | bytes 1081352 | tf_op jit(solution)/shard_map/ppermute | solution.py:428
  15.5 1.1 %collective-permute-done.1.refs_1_.refs_2_ = bf16[1,128,1408]{2,1,0:T(8,128)(2,1)S(1)} collective-permute-done((bf16[1,128,1408]{2,1,0:T(8,128)(2,1)}, bf16[1,128,1408]{2,1,0:T(8,128)(2,1)S(1)}, u32[]{:S(2)}, u32[]{:S(2)}) %collective-permute-start.1) | collective-permute-done | bytes 360480 | tf_op jit(solution)/shard_map/ppermute | solution.py:424
  19.3 1.8 %image_group.4 = (bf16[1,32,512]{2,1,0:T(8,128)(2,1)S(1)}, bf16[1,32,512]{2,1,0:T(8,128)(2,1)S(1)}, bf16[128,1024]{1,0:T(8,128)(2,1)S(1)}, bf16[1,4,176,128]{3,2...) custom-call(s32[2]{0:T(128)S(1)} %pad_add_fusion.ids, s32[4]{0:T(128)S(1)} %copy-done.6, bf16[1,128,1408]{2,1,0:T(8,128)(2,1)S(1)} %copy-done.5, ...), custom_call_target="tpu_custom_call" | custom-call | tf_op jit(solution)/shard_map/image_group/pallas_call | solution.py:108
  21.7 2.5 %collective-permute-done.2.refs_0_ = bf16[1,128,1408]{2,1,0:T(8,128)(2,1)S(1)} collective-permute-done((bf16[1,128,1408]{2,1,0:T(8,128)(2,1)}, bf16[1,128,1408]{2,1,0:T(8,128)(2,1)S(1)}, u32[]{:S(2)}, u32[]{:S(2)}) %collective-permute-start.2) | collective-permute-done | bytes 360480 | tf_op jit(solution)/shard_map/ppermute | solution.py:426
  24.2 1.8 %image_group.6 = (bf16[1,32,512]{2,1,0:T(8,128)(2,1)S(1)}, bf16[1,32,512]{2,1,0:T(8,128)(2,1)S(1)}, bf16[128,1024]{1,0:T(8,128)(2,1)S(1)}, bf16[1,4,176,128]{3,2...) custom-call(s32[2]{0:T(128)S(1)} %pad_add_fusion.ids, s32[4]{0:T(128)S(1)} %copy-done.6, ...), custom_call_target="tpu_custom_call" | custom-call | tf_op jit(solution)/shard_map/image_group/pallas_call | solution.py:108
  26.1 1.8 %image_group.5 = (bf16[1,32,512]{2,1,0:T(8,128)(2,1)S(1)}, bf16[1,32,512]{2,1,0:T(8,128)(2,1)S(1)}, bf16[128,1024]{1,0:T(8,128)(2,1)S(1)}, bf16[1,4,176,128]{3,2...) custom-call(s32[2]{0:T(128)S(1)} %pad_add_fusion.ids, s32[4]{0:T(128)S(1)} %copy-done.6, ...), custom_call_target="tpu_custom_call" | custom-call | tf_op jit(solution)/shard_map/image_group/pallas_call | solution.py:108
  28.0 3.9 %collective-permute-done.3.refs_0_ = bf16[1,128,1408]{2,1,0:T(8,128)(2,1)S(1)} collective-permute-done((bf16[1,128,1408]{2,1,0:T(8,128)(2,1)S(1)}, bf16[1,128,1408]{2,1,0:T(8,128)(2,1)S(1)}, u32[]{:S(2)}, u32[]{:S(2)}) %collective-permute-start.3) | collective-permute-done | bytes 360480 | tf_op jit(solution)/shard_map/ppermute | solution.py:428
  32.4 1.8 %image_group.7 = (bf16[1,32,512]{2,1,0:T(8,128)(2,1)S(1)}, bf16[1,32,512]{2,1,0:T(8,128)(2,1)S(1)}, bf16[128,1024]{1,0:T(8,128)(2,1)S(1)}, bf16[1,4,176,128]{3,2...) custom-call(s32[2]{0:T(128)S(1)} %pad_add_fusion.ids, s32[4]{0:T(128)S(1)} %copy-done.6, ...), custom_call_target="tpu_custom_call" | custom-call | tf_op jit(solution)/shard_map/image_group/pallas_call | solution.py:108
  34.9 1.2 %collective-permute-done.8.refs_4_ = bf16[1,4,176,128]{3,2,1,0:T(8,128)(2,1)S(1)} collective-permute-done((bf16[1,4,176,128]{3,2,1,0:T(8,128)(2,1)S(1)}, bf16[1,4,176,128]{3,2,1,0:T(8,128)(2,1)S(1)}, u32[]{:S(2)}, u32[]{:S(2)}) %collective-permute-start.8) | collective-permute-done | bytes 180256 | tf_op jit(solution)/shard_map/ppermute | solution.py:407
  36.1 1.4 %early_terms.1.refs_4_ = f32[4,176,1024]{2,1,0:T(8,128)S(1)} custom-call(bf16[1,4,176,128]{3,2,1,0:T(8,128)(2,1)S(1)} %get-tuple-element.47.refs_0_, bf16[1,4,176,128]{3,2,1,0:T(8,128)(2,1)S(1)} %get-tuple-element.48.refs_1_, bf16[1,4,176,128]{3,2,1,0:T(8,128)(2,1)S(1)} %get-tuple-element.49.refs_2_, ...), custom_call_target="tpu_custom_call" | custom-call | tf_op jit(solution)/shard_map/early_terms/pallas_call | solution.py:142
  37.4 0.8 weight_terms.3
  38.3 2.5 %collective-permute-start.13 = (bf16[176,1024]{1,0:T(8,128)(2,1)S(1)}, bf16[176,1024]{1,0:T(8,128)(2,1)S(1)}, u32[]{:S(2)}, u32[]{:S(2)}) collective-permute-start(bf16[176,1024]{1,0:T(8,128)(2,1)S(1)} %weight_terms.3), channel_id=1, source_target_pairs={{0,24},{4,28},{8,16},{12,20},{16,8},{20,12},{24,0},{28,4},{1,25},{... | collective-permute-start | bytes 1081352 | tf_op jit(solution)/shard_map/ppermute | solution.py:407
  40.8 1.0 %weight_terms.2 = (bf16[176,1024]{1,0:T(8,128)(2,1)S(1)}, bf16[176,1024]{1,0:T(8,128)(2,1)S(1)}, f32[176,1024]{1,0:T(8,128)S(1)}) custom-call(s32[2]{0:T(128)S(1)} %pad_add_fusion.ids, bf16[1,4,176,128]{3,2,1,0:T(8,128)(2,1)S(1)} %get-tuple-element.44.refs_0_, bf16[1,4,176,128]{3,2,1,0:T(8,128)(2,1)S(1)} %collective-permute-done.5.refs_1_, ...), custom_call_target="tpu_custom_call" | custom-call | tf_op jit(solution)/shard_map/weight_terms/pallas_call | solution.py:167
  43.0 1.2 %collective-permute-done.16.second = bf16[1,3456]{1,0:T(2,128)(2,1)S(1)} collective-permute-done((bf16[1,3456]{1,0:T(2,128)(2,1)S(1)}, bf16[1,3456]{1,0:T(2,128)(2,1)S(1)}, u32[]{:S(2)}, u32[]{:S(2)}) %collective-permute-start.16) | collective-permute-done | bytes 6944 | tf_op jit(solution)/shard_map/ppermute | solution.py:407
  44.2 1.6 %collective-permute-start.17 = (bf16[2,3456]{1,0:T(2,128)(2,1)S(1)}, bf16[2,3456]{1,0:T(2,128)(2,1)S(1)}, u32[]{:S(2)}, u32[]{:S(2)}) collective-permute-start(bf16[2,3456]{1,0:T(2,128)(2,1)S(1)} %append.3.first), channel_id=1, source_target_pairs={{0,8},{4,12},{8,0},{12,4},{16,24},{20,28},{24,16},{28,20},{1,9},{5... | collective-permute-start | bytes 41480 | tf_op jit(solution)/shard_map/ppermute | solution.py:407
  45.8 12.1 %collective-permute-done.17.second = bf16[2,3456]{1,0:T(2,128)(2,1)S(1)} collective-permute-done((bf16[2,3456]{1,0:T(2,128)(2,1)S(1)}, bf16[2,3456]{1,0:T(2,128)(2,1)S(1)}, u32[]{:S(2)}, u32[]{:S(2)}) %collective-permute-start.17) | collective-permute-done | bytes 13856 | tf_op jit(solution)/shard_map/ppermute | solution.py:407
  58.4 3.4 %collective-permute-done.18.second = bf16[4,3456]{1,0:T(4,128)(2,1)S(1)} collective-permute-done((bf16[4,3456]{1,0:T(4,128)(2,1)S(1)}, bf16[4,3456]{1,0:T(4,128)(2,1)S(1)}, u32[]{:S(2)}, u32[]{:S(2)}) %collective-permute-start.18) | collective-permute-done | bytes 27680 | tf_op jit(solution)/shard_map/ppermute | solution.py:407
  61.8 6.0 %collective-permute-start.19 = (bf16[8,1408]{1,0:T(8,128)(2,1)S(1)}, bf16[8,1408]{1,0:T(8,128)(2,1)S(1)}, u32[]{:S(2)}, u32[]{:S(2)}) collective-permute-start(bf16[8,1408]{1,0:T(8,128)(2,1)S(1)} %get-tuple-element.62), channel_id=1, source_target_pairs={{0,1},{1,0},{2,3},{3,2},{4,5},{5,4},{6,7},{7,6},{8,9},{9,8},{10,11... | collective-permute-start | bytes 67592 | tf_op jit(solution)/shard_map/ppermute | solution.py:407
  67.8 1.2 %collective-permute-start.20 = (bf16[8,1408]{1,0:T(8,128)(2,1)S(1)}, bf16[8,1408]{1,0:T(8,128)(2,1)S(1)}, u32[]{:S(2)}, u32[]{:S(2)}) collective-permute-start(bf16[8,1408]{1,0:T(8,128)(2,1)S(1)} %get-tuple-element.62), channel_id=1, source_target_pairs={{0,2},{1,3},{2,0},{3,1},{4,6},{5,7},{6,4},{7,5},{8,10},{9,11},{10,... | collective-permute-start | bytes 67592 | tf_op jit(solution)/shard_map/ppermute | solution.py:407
  69.8 2.6 %collective-permute-start.21 = (bf16[8,1408]{1,0:T(8,128)(2,1)S(1)}, bf16[8,1408]{1,0:T(8,128)(2,1)S(1)}, u32[]{:S(2)}, u32[]{:S(2)}) collective-permute-start(bf16[8,1408]{1,0:T(8,128)(2,1)S(1)} %get-tuple-element.62), channel_id=1, source_target_pairs={{0,3},{1,2},{2,1},{3,0},{4,7},{5,6},{6,5},{7,4},{8,11},{9,10},{10,... | collective-permute-start | bytes 67592 | tf_op jit(solution)/shard_map/ppermute | solution.py:407
  72.7 2.8 %collective-permute-done.21.refs_3_ = bf16[8,1408]{1,0:T(8,128)(2,1)S(1)} collective-permute-done((bf16[8,1408]{1,0:T(8,128)(2,1)S(1)}, bf16[8,1408]{1,0:T(8,128)(2,1)S(1)}, u32[]{:S(2)}, u32[]{:S(2)}) %collective-permute-start.21) | collective-permute-done | bytes 22560 | tf_op jit(solution)/shard_map/ppermute | solution.py:407
  75.5 1.0 %similarity_terms.1.refs_1_ = f32[32,34]{1,0:T(8,128)S(1)} custom-call(s32[2]{0:T(128)S(1)} %pad_add_fusion.ids, bf16[8,3456]{1,0:T(8,128)(2,1)S(1)} %get-tuple-element.61.refs_0_, bf16[8,1408]{1,0:T(8,128)(2,1)S(1)} %collective-permute-done.19.refs_1_, bf16[8,1408]{1,0:T(8,128)(2,1)S(1)} %collective-permute-done.20.refs_2_, ...), custom_call_target="tpu_custom_call" | custom-call | tf_op jit(solution)/shard_map/similarity_terms/pallas_call | solution.py:319
  76.6 3.2 %collective-permute-start.23 = (f32[32,34]{1,0:T(8,128)S(1)}, f32[32,34]{1,0:T(8,128)S(1)}, u32[]{:S(2)}, u32[]{:S(2)}) collective-permute-start(f32[32,34]{1,0:T(8,128)S(1)} %similarity_terms.1.refs_1_), channel_id=1, source_target_pairs={{0,2},{1,3},{2,0},{3,1},{4,6},{5,7},{6,4},{7,5},{8,10},{9,11},{10,... | collective-permute-start | bytes 13064 | tf_op jit(solution)/shard_map/ppermute | solution.py:407
  80.3 2.7 %collective-permute-start.24 = (f32[32,34]{1,0:T(8,128)S(1)}, f32[32,34]{1,0:T(8,128)S(1)}, u32[]{:S(2)}, u32[]{:S(2)}) collective-permute-start(f32[32,34]{1,0:T(8,128)S(1)} %similarity_terms.1.refs_1_), channel_id=1, source_target_pairs={{0,3},{1,2},{2,1},{3,0},{4,7},{5,6},{6,5},{7,4},{8,11},{9,10},{10,... | collective-permute-start | bytes 13064 | tf_op jit(solution)/shard_map/ppermute | solution.py:407
  83.6 2.2 %collective-permute-done.24.refs_4_ = f32[32,34]{1,0:T(8,128)S(1)} collective-permute-done((f32[32,34]{1,0:T(8,128)S(1)}, f32[32,34]{1,0:T(8,128)S(1)}, u32[]{:S(2)}, u32[]{:S(2)}) %collective-permute-start.24) | collective-permute-done | bytes 4384 | tf_op jit(solution)/shard_map/ppermute | solution.py:407
  85.8 1.4 %losses.1 = f32[2,4]{1,0:T(2,128)} custom-call(s32[2]{0:T(128)S(1)} %pad_add_fusion.ids, f32[1]{0:T(128)S(6)} %copy.15.refs_0_, f32[32,34]{1,0:T(8,128)S(1)} %similarity_terms.1.refs_1_, f32[32,34]{1,0:T(8,128)S(1)} %collective-permute-done.22.refs_2_, f32[32,34]{1,0:T(8,128)S(1)} %collective-permute-done.23.refs_3_, ...), custom_call_target="tpu_custom_call" | custom-call | tf_op jit(solution)/shard_map/losses/pallas_call | solution.py:391
  87.3 1.3 %arrange.1 = (bf16[4,32,512]{2,1,0:T(8,128)(2,1)}, bf16[4,32,512]{2,1,0:T(8,128)(2,1)}) custom-call(s32[2]{0:T(128)S(1)} %pad_add_fusion.ids, bf16[1,32,512]{2,1,0:T(8,128)(2,1)S(1)} %get-tuple-element.34.refs_0_, bf16[1,32,512]{2,1,0:T(8,128)(2,1)S(1)} %get-tuple-element.35.refs_1_, bf16[1,32,512]{2,1,0:T(8,128)(2,1)S(1)} %get-tuple-element.36.refs_2_, ...), custom_call_target="tpu_custom_call" | custom-call | tf_op jit(solution)/shard_map/arrange/pallas_call | solution.py:221
  88.5 0.9 %finish.1 = (f32[176,512]{1,0:T(8,128)}, f32[176,512]{1,0:T(8,128)}) custom-call(f32[176,1024]{1,0:T(8,128)S(1)} %get-tuple-element.56.refs_0_, bf16[176,1024]{1,0:T(8,128)(2,1)S(1)} %collective-permute-done.13.refs_1_, bf16[176,1024]{1,0:T(8,128)(2,1)S(1)} %collective-permute-done.14.refs_2_, bf16[176,1024]{1,0:T(8,128)(2,1)S(1)} %collective-permute-done.15.refs_3_), custom_call_target="tpu_custom_call" | custom-call | tf_op jit(solution)/shard_map/finish/pallas_call | solution.py:200
  (53 shorter events, 7.9 us)
Async XLA Ops:
  0.6 13.6 %collective-permute-start = (bf16[1,128,1408]{2,1,0:T(8,128)(2,1)}, bf16[1,128,1408]{2,1,0:T(8,128)(2,1)S(1)}, u32[]{:S(2)}, u32[]{:S(2)}) collective-permute-start(bf16[1,128,1408]{2,1,0:T(8,128)(2,1)} %refs_0_.2), channel_id=1, source_target_pairs={{1,0},{2,1},{3,2},{5,4},{6,5},{7,6},{9,8},{10,9},{11,10},{13,12},{... | collective-permute-start | bytes 1081352 | tf_op jit(solution)/shard_map/ppermute | solution.py:425
  1.9 14.7 %collective-permute-start.1 = (bf16[1,128,1408]{2,1,0:T(8,128)(2,1)}, bf16[1,128,1408]{2,1,0:T(8,128)(2,1)S(1)}, u32[]{:S(2)}, u32[]{:S(2)}) collective-permute-start(bf16[1,128,1408]{2,1,0:T(8,128)(2,1)} %refs_0_.2), channel_id=1, source_target_pairs={{0,1},{1,2},{2,3},{4,5},{5,6},{6,7},{8,9},{9,10},{10,11},{12,13},{... | collective-permute-start | bytes 1081352 | tf_op jit(solution)/shard_map/ppermute | solution.py:424
  7.5 16.7 %collective-permute-start.2 = (bf16[1,128,1408]{2,1,0:T(8,128)(2,1)}, bf16[1,128,1408]{2,1,0:T(8,128)(2,1)S(1)}, u32[]{:S(2)}, u32[]{:S(2)}) collective-permute-start(bf16[1,128,1408]{2,1,0:T(8,128)(2,1)} %refs_0_.2), channel_id=1, source_target_pairs={{0,3},{3,0},{4,7},{7,4},{8,11},{11,8},{12,15},{15,12},{16,19},{19,... | collective-permute-start | bytes 1081352 | tf_op jit(solution)/shard_map/ppermute | solution.py:426
  14.2 17.6 %collective-permute-start.3 = (bf16[1,128,1408]{2,1,0:T(8,128)(2,1)S(1)}, bf16[1,128,1408]{2,1,0:T(8,128)(2,1)S(1)}, u32[]{:S(2)}, u32[]{:S(2)}) collective-permute-start(bf16[1,128,1408]{2,1,0:T(8,128)(2,1)S(1)} %collective-permute-done.refs_0_.refs_1_), channel_id=1, source_target_pairs={{1,0},{2,1},{5,4},{6,5},{9,8},{10,9},{13,12},{14,13},{17,16},{18,1... | collective-permute-start | bytes 1081352 | tf_op jit(solution)/shard_map/ppermute | solution.py:428
  16.6 15.2 %collective-permute-start.4 = (bf16[1,128,1408]{2,1,0:T(8,128)(2,1)S(1)}, bf16[1,128,1408]{2,1,0:T(8,128)(2,1)S(1)}, u32[]{:S(2)}, u32[]{:S(2)}) collective-permute-start(bf16[1,128,1408]{2,1,0:T(8,128)(2,1)S(1)} %collective-permute-done.1.refs_1_.refs_2_), channel_id=1, source_target_pairs={{1,2},{2,3},{5,6},{6,7},{9,10},{10,11},{13,14},{14,15},{17,18},{18... | collective-permute-start | bytes 1081352 | tf_op jit(solution)/shard_map/ppermute | solution.py:427
  17.4 1.8 %copy-start.2 = (bf16[4,32,512]{2,1,0:T(8,128)(2,1)S(1)}, bf16[4,32,512]{2,1,0:T(8,128)(2,1)}, u32[]{:S(2)}) copy-start(bf16[4,32,512]{2,1,0:T(8,128)(2,1)} %refs_5_.7) | copy-start | bytes 393220
  17.4 1.8 %copy-start.3 = (bf16[4,32,512]{2,1,0:T(8,128)(2,1)S(1)}, bf16[4,32,512]{2,1,0:T(8,128)(2,1)}, u32[]{:S(2)}) copy-start(bf16[4,32,512]{2,1,0:T(8,128)(2,1)} %refs_6_.5) | copy-start | bytes 393220
  17.4 1.9 %copy-start.5 = (bf16[1,128,1408]{2,1,0:T(8,128)(2,1)S(1)}, bf16[1,128,1408]{2,1,0:T(8,128)(2,1)}, u32[]{:S(2)}) copy-start(bf16[1,128,1408]{2,1,0:T(8,128)(2,1)} %refs_0_.2) | copy-start | bytes 1081348
  17.4 1.9 %copy-start.6 = (s32[4]{0:T(128)S(1)}, s32[4]{0:T(128)}, u32[]{:S(2)}) copy-start(s32[4]{0:T(128)} %lens.7) | copy-start | bytes 52
  21.1 13.2 %collective-permute-start.10 = (bf16[128,1024]{1,0:T(8,128)(2,1)S(1)}, bf16[128,1024]{1,0:T(8,128)(2,1)S(1)}, u32[]{:S(2)}, u32[]{:S(2)}) collective-permute-start(bf16[128,1024]{1,0:T(8,128)(2,1)S(1)} %get-tuple-element.53.refs_6_), channel_id=1, source_target_pairs={{0,4},{4,0},{8,12},{12,8},{16,20},{20,16},{24,28},{28,24},{1,5},{5... | collective-permute-start | bytes 786440 | tf_op jit(solution)/shard_map/ppermute | solution.py:407
  21.2 13.0 %collective-permute-start.7 = (bf16[1,4,176,128]{3,2,1,0:T(8,128)(2,1)S(1)}, bf16[1,4,176,128]{3,2,1,0:T(8,128)(2,1)S(1)}, u32[]{:S(2)}, u32[]{:S(2)}) collective-permute-start(bf16[1,4,176,128]{3,2,1,0:T(8,128)(2,1)S(1)} %get-tuple-element.50), channel_id=1, source_target_pairs={{0,4},{4,0},{8,12},{12,8},{16,20},{20,16},{24,28},{28,24},{1,5},{5... | collective-permute-start | bytes 540680 | tf_op jit(solution)/shard_map/ppermute | solution.py:407
  26.0 8.7 %collective-permute-start.9 = (bf16[1,4,176,128]{3,2,1,0:T(8,128)(2,1)S(1)}, bf16[1,4,176,128]{3,2,1,0:T(8,128)(2,1)S(1)}, u32[]{:S(2)}, u32[]{:S(2)}) collective-permute-start(bf16[1,4,176,128]{3,2,1,0:T(8,128)(2,1)S(1)} %get-tuple-element.52), channel_id=1, source_target_pairs={{0,4},{4,0},{8,12},{12,8},{16,20},{20,16},{24,28},{28,24},{1,5},{5... | collective-permute-start | bytes 540680 | tf_op jit(solution)/shard_map/ppermute | solution.py:407
  31.8 4.2 %collective-permute-start.12 = (bf16[128,1024]{1,0:T(8,128)(2,1)S(1)}, bf16[128,1024]{1,0:T(8,128)(2,1)S(1)}, u32[]{:S(2)}, u32[]{:S(2)}) collective-permute-start(bf16[128,1024]{1,0:T(8,128)(2,1)S(1)} %get-tuple-element.55.refs_8_), channel_id=1, source_target_pairs={{0,4},{4,0},{8,12},{12,8},{16,20},{20,16},{24,28},{28,24},{1,5},{5... | collective-permute-start | bytes 786440 | tf_op jit(solution)/shard_map/ppermute | solution.py:407
  31.9 4.2 %collective-permute-start.11 = (bf16[128,1024]{1,0:T(8,128)(2,1)S(1)}, bf16[128,1024]{1,0:T(8,128)(2,1)S(1)}, u32[]{:S(2)}, u32[]{:S(2)}) collective-permute-start(bf16[128,1024]{1,0:T(8,128)(2,1)S(1)} %get-tuple-element.54.refs_7_), channel_id=1, source_target_pairs={{0,4},{4,0},{8,12},{12,8},{16,20},{20,16},{24,28},{28,24},{1,5},{5... | collective-permute-start | bytes 786440 | tf_op jit(solution)/shard_map/ppermute | solution.py:407
  34.2 3.2 %collective-permute-start.6 = (bf16[128,1024]{1,0:T(8,128)(2,1)S(1)}, bf16[128,1024]{1,0:T(8,128)(2,1)S(1)}, u32[]{:S(2)}, u32[]{:S(2)}) collective-permute-start(bf16[128,1024]{1,0:T(8,128)(2,1)S(1)} %get-tuple-element.46.refs_2_), channel_id=1, source_target_pairs={{0,4},{4,0},{8,12},{12,8},{16,20},{20,16},{24,28},{28,24},{1,5},{5... | collective-permute-start | bytes 786440 | tf_op jit(solution)/shard_map/ppermute | solution.py:407
  34.3 1.8 %collective-permute-start.8 = (bf16[1,4,176,128]{3,2,1,0:T(8,128)(2,1)S(1)}, bf16[1,4,176,128]{3,2,1,0:T(8,128)(2,1)S(1)}, u32[]{:S(2)}, u32[]{:S(2)}) collective-permute-start(bf16[1,4,176,128]{3,2,1,0:T(8,128)(2,1)S(1)} %get-tuple-element.51), channel_id=1, source_target_pairs={{0,4},{4,0},{8,12},{12,8},{16,20},{20,16},{24,28},{28,24},{1,5},{5... | collective-permute-start | bytes 540680 | tf_op jit(solution)/shard_map/ppermute | solution.py:407
  34.8 2.7 %collective-permute-start.5 = (bf16[1,4,176,128]{3,2,1,0:T(8,128)(2,1)S(1)}, bf16[1,4,176,128]{3,2,1,0:T(8,128)(2,1)S(1)}, u32[]{:S(2)}, u32[]{:S(2)}) collective-permute-start(bf16[1,4,176,128]{3,2,1,0:T(8,128)(2,1)S(1)} %get-tuple-element.45), channel_id=1, source_target_pairs={{0,4},{4,0},{8,12},{12,8},{16,20},{20,16},{24,28},{28,24},{1,5},{5... | collective-permute-start | bytes 540680 | tf_op jit(solution)/shard_map/ppermute | solution.py:407
  38.3 4.7 %copy-start.7 = (bf16[1,1408]{1,0:T(2,128)(2,1)S(1)}, bf16[1,1408]{1,0:T(2,128)(2,1)}, u32[]{:S(2)}) copy-start(bf16[1,1408]{1,0:T(2,128)(2,1)} %pooled.1) | copy-start | bytes 8452
  38.3 4.7 %copy-start.8 = (bf16[4,512]{1,0:T(4,128)(2,1)S(1)}, bf16[4,512]{1,0:T(4,128)(2,1)}, u32[]{:S(2)}) copy-start(bf16[4,512]{1,0:T(4,128)(2,1)} %texts.1) | copy-start | bytes 12292
  38.3 37.2 %copy-start.4 = (bf16[1408,512]{1,0:T(8,128)(2,1)S(1)}, bf16[1408,512]{1,0:T(8,128)(2,1)}, u32[]{:S(2)}) copy-start(bf16[1408,512]{1,0:T(8,128)(2,1)} %refs_4_.9) | copy-start | bytes 4325380
  38.3 50.2 %collective-permute-start.13 = (bf16[176,1024]{1,0:T(8,128)(2,1)S(1)}, bf16[176,1024]{1,0:T(8,128)(2,1)S(1)}, u32[]{:S(2)}, u32[]{:S(2)}) collective-permute-start(bf16[176,1024]{1,0:T(8,128)(2,1)S(1)} %weight_terms.3), channel_id=1, source_target_pairs={{0,24},{4,28},{8,16},{12,20},{16,8},{20,12},{24,0},{28,4},{1,25},{... | collective-permute-start | bytes 1081352 | tf_op jit(solution)/shard_map/ppermute | solution.py:407
  41.8 46.8 %collective-permute-start.14 = (bf16[176,1024]{1,0:T(8,128)(2,1)S(1)}, bf16[176,1024]{1,0:T(8,128)(2,1)S(1)}, u32[]{:S(2)}, u32[]{:S(2)}) collective-permute-start(bf16[176,1024]{1,0:T(8,128)(2,1)S(1)} %get-tuple-element.57), channel_id=1, source_target_pairs={{0,16},{4,20},{8,24},{12,28},{16,0},{20,4},{24,8},{28,12},{1,17},{... | collective-permute-start | bytes 1081352 | tf_op jit(solution)/shard_map/ppermute | solution.py:407
  42.4 46.1 %collective-permute-start.15 = (bf16[176,1024]{1,0:T(8,128)(2,1)S(1)}, bf16[176,1024]{1,0:T(8,128)(2,1)S(1)}, u32[]{:S(2)}, u32[]{:S(2)}) collective-permute-start(bf16[176,1024]{1,0:T(8,128)(2,1)S(1)} %get-tuple-element.58), channel_id=1, source_target_pairs={{0,8},{4,12},{8,0},{12,4},{16,24},{20,28},{24,16},{28,20},{1,9},{5... | collective-permute-start | bytes 1081352 | tf_op jit(solution)/shard_map/ppermute | solution.py:407
  42.9 1.2 %collective-permute-start.16 = (bf16[1,3456]{1,0:T(2,128)(2,1)S(1)}, bf16[1,3456]{1,0:T(2,128)(2,1)S(1)}, u32[]{:S(2)}, u32[]{:S(2)}) collective-permute-start(bf16[1,3456]{1,0:T(2,128)(2,1)S(1)} %join_facts.1.first), channel_id=1, source_target_pairs={{0,4},{4,0},{8,12},{12,8},{16,20},{20,16},{24,28},{28,24},{1,5},{5... | collective-permute-start | bytes 20744 | tf_op jit(solution)/shard_map/ppermute | solution.py:407
  44.2 13.7 %collective-permute-start.17 = (bf16[2,3456]{1,0:T(2,128)(2,1)S(1)}, bf16[2,3456]{1,0:T(2,128)(2,1)S(1)}, u32[]{:S(2)}, u32[]{:S(2)}) collective-permute-start(bf16[2,3456]{1,0:T(2,128)(2,1)S(1)} %append.3.first), channel_id=1, source_target_pairs={{0,8},{4,12},{8,0},{12,4},{16,24},{20,28},{24,16},{28,20},{1,9},{5... | collective-permute-start | bytes 41480 | tf_op jit(solution)/shard_map/ppermute | solution.py:407
  57.9 3.9 %collective-permute-start.18 = (bf16[4,3456]{1,0:T(4,128)(2,1)S(1)}, bf16[4,3456]{1,0:T(4,128)(2,1)S(1)}, u32[]{:S(2)}, u32[]{:S(2)}) collective-permute-start(bf16[4,3456]{1,0:T(4,128)(2,1)S(1)} %append.4.first), channel_id=1, source_target_pairs={{0,16},{4,20},{8,24},{12,28},{16,0},{20,4},{24,8},{28,12},{1,17},{... | collective-permute-start | bytes 82952 | tf_op jit(solution)/shard_map/ppermute | solution.py:407
  61.8 8.0 %collective-permute-start.19 = (bf16[8,1408]{1,0:T(8,128)(2,1)S(1)}, bf16[8,1408]{1,0:T(8,128)(2,1)S(1)}, u32[]{:S(2)}, u32[]{:S(2)}) collective-permute-start(bf16[8,1408]{1,0:T(8,128)(2,1)S(1)} %get-tuple-element.62), channel_id=1, source_target_pairs={{0,1},{1,0},{2,3},{3,2},{4,5},{5,4},{6,7},{7,6},{8,9},{9,8},{10,11... | collective-permute-start | bytes 67592 | tf_op jit(solution)/shard_map/ppermute | solution.py:407
  67.8 4.9 %collective-permute-start.20 = (bf16[8,1408]{1,0:T(8,128)(2,1)S(1)}, bf16[8,1408]{1,0:T(8,128)(2,1)S(1)}, u32[]{:S(2)}, u32[]{:S(2)}) collective-permute-start(bf16[8,1408]{1,0:T(8,128)(2,1)S(1)} %get-tuple-element.62), channel_id=1, source_target_pairs={{0,2},{1,3},{2,0},{3,1},{4,6},{5,7},{6,4},{7,5},{8,10},{9,11},{10,... | collective-permute-start | bytes 67592 | tf_op jit(solution)/shard_map/ppermute | solution.py:407
  69.8 5.6 %collective-permute-start.21 = (bf16[8,1408]{1,0:T(8,128)(2,1)S(1)}, bf16[8,1408]{1,0:T(8,128)(2,1)S(1)}, u32[]{:S(2)}, u32[]{:S(2)}) collective-permute-start(bf16[8,1408]{1,0:T(8,128)(2,1)S(1)} %get-tuple-element.62), channel_id=1, source_target_pairs={{0,3},{1,2},{2,1},{3,0},{4,7},{5,6},{6,5},{7,4},{8,11},{9,10},{10,... | collective-permute-start | bytes 67592 | tf_op jit(solution)/shard_map/ppermute | solution.py:407
  76.5 3.8 %collective-permute-start.22 = (f32[32,34]{1,0:T(8,128)S(1)}, f32[32,34]{1,0:T(8,128)S(1)}, u32[]{:S(2)}, u32[]{:S(2)}) collective-permute-start(f32[32,34]{1,0:T(8,128)S(1)} %similarity_terms.1.refs_1_), channel_id=1, source_target_pairs={{0,1},{1,0},{2,3},{3,2},{4,5},{5,4},{6,7},{7,6},{8,9},{9,8},{10,11... | collective-permute-start | bytes 13064 | tf_op jit(solution)/shard_map/ppermute | solution.py:407
  76.6 7.1 %collective-permute-start.23 = (f32[32,34]{1,0:T(8,128)S(1)}, f32[32,34]{1,0:T(8,128)S(1)}, u32[]{:S(2)}, u32[]{:S(2)}) collective-permute-start(f32[32,34]{1,0:T(8,128)S(1)} %similarity_terms.1.refs_1_), channel_id=1, source_target_pairs={{0,2},{1,3},{2,0},{3,1},{4,6},{5,7},{6,4},{7,5},{8,10},{9,11},{10,... | collective-permute-start | bytes 13064 | tf_op jit(solution)/shard_map/ppermute | solution.py:407
  80.3 5.5 %collective-permute-start.24 = (f32[32,34]{1,0:T(8,128)S(1)}, f32[32,34]{1,0:T(8,128)S(1)}, u32[]{:S(2)}, u32[]{:S(2)}) collective-permute-start(f32[32,34]{1,0:T(8,128)S(1)} %similarity_terms.1.refs_1_), channel_id=1, source_target_pairs={{0,3},{1,2},{2,1},{3,0},{4,7},{5,6},{6,5},{7,4},{8,11},{9,10},{10,... | collective-permute-start | bytes 13064 | tf_op jit(solution)/shard_map/ppermute | solution.py:407
  (2 other events, 3.2 us)

commit v2 on v1

--- a/solution.py
+++ b/solution.py
@@ -121,7 +121,6 @@
         ),
         out_shape=results,
         compiler_params=room(*operands, *results, operands[0]),
-        name="image_group",
     )(ids, lengths, *operands)
 
 
@@ -143,7 +142,6 @@
         functools.partial(early_kernel, len(turned)),
         out_shape=result,
         compiler_params=room(*turned, *grads, result),
-        name="early_terms",
     )(*turned, *grads)
 
 
@@ -174,13 +172,96 @@
         ),
         out_shape=results,
         compiler_params=room(*turned, *grads, *results, early),
-        name="weight_terms",
     )(ids, *turned, *grads, early)
 
 
 def one_kernel(count, piece, ids, *refs):
     turned, grads, early, out = refs[:count], refs[count : 2 * count], *refs[2 * count :]
     out[...] = (early[0] + joined(turned, grads, (ids[0] >> 1) ^ piece)).astype(out.dtype)
+
+
+def part_kernel(count, wanted, ids, *refs):
+    turned, grads, early = refs[:count], refs[count : 2 * count], refs[2 * count]
+    outs = refs[2 * count + 1 :]
+    width = early.shape[2] // 2
+    for side in range(2):
+        cols = slice(side * width, (side + 1) * width)
+        needs = [(o, i, m) for o, w in enumerate(wanted) for i, (m, h) in enumerate(w) if h == side]
+        if not needs:
+            continue
+        right = jnp.concatenate([g[:, cols] for g in grads])
+        for o, i, m in needs:
+            place = (ids[0] >> 1) ^ m
+            left = jnp.concatenate(
+                [t[n, place] for t in turned for n in range(t.shape[0])], axis=1
+            )
+            total = early[place, :, cols] + jnp.dot(left, right, preferred_element_type=F32)
+            outs[o][i] = total.astype(outs[o].dtype)
+
+
+def term_parts(ids, wanted, dtype, turned, grads, early):
+    rows, width = early.shape[1], early.shape[2] // 2
+    full = lambda shape: pl.BlockSpec(shape, lambda i, o: (0,) * len(shape))
+    operands = [*turned, *grads, early]
+    results = [jax.ShapeDtypeStruct((len(w), rows, width), dtype) for w in wanted]
+    return pl.pallas_call(
+        functools.partial(part_kernel, len(turned), wanted),
+        grid_spec=pltpu.PrefetchScalarGridSpec(
+            num_scalar_prefetch=1,
+            grid=(1,),
+            in_specs=[full(o.shape) for o in operands],
+            out_specs=[full(r.shape) for r in results],
+        ),
+        out_shape=results,
+        compiler_params=room(*operands, *results),
+    )(ids, *operands)
+
+
+def pass_kernel(side, kept, got, out):
+    out[...] = (kept[side] + got[1].astype(F32)).astype(out.dtype)
+
+
+def pass_on(side, kept, got):
+    return pl.pallas_call(
+        functools.partial(pass_kernel, side),
+        out_shape=jax.ShapeDtypeStruct(kept.shape[1:], BF16),
+        compiler_params=room(kept, got, got),
+    )(kept, got)
+
+
+def half_finish_kernel(side, own, first, second, out):
+    out[...] = own[side] + first[0].astype(F32) + second[...].astype(F32)
+
+
+def half_finish(side, own, first, second):
+    return pl.pallas_call(
+        functools.partial(half_finish_kernel, side),
+        out_shape=jax.ShapeDtypeStruct(own.shape[1:], F32),
+        compiler_params=room(own, first, second),
+    )(own, first, second)
+
+
+def direct_sums(ids, n_dp, sides):
+    half = n_dp // 2
+    (last,) = weight_terms(ids, (half - 1,), *sides)
+    arrived = [flip(last, "dp", n_dp, 2 * (half - 1))]
+    pieces = weight_terms(ids, tuple(range(half - 2, -1, -1)), *sides)
+    for m, piece in zip(range(half - 2, 0, -1), pieces):
+        arrived.append(flip(piece, "dp", n_dp, 2 * m))
+    return finish(pieces[-1], arrived)
+
+
+def staged_sums(ids, n_dp, sides):
+    key_send, value_send = term_parts(ids, [[(1, 0), (3, 0)], [(2, 1), (3, 1)]], BF16, *sides)
+    key_1 = flip(key_send, "dp", n_dp, 2)
+    value_1 = flip(value_send, "dp", n_dp, 4)
+    own, kept = term_parts(ids, [[(0, 0), (0, 1)], [(2, 0), (1, 1)]], F32, *sides)
+    key_on = pass_on(0, kept, key_1)
+    key_2 = flip(key_on, "dp", n_dp, 4)
+    value_on = pass_on(1, kept, value_1)
+    value_2 = flip(value_on, "dp", n_dp, 2)
+    dw_key = half_finish(0, own, key_1, key_2)
+    return dw_key, half_finish(1, own, value_1, value_2)
 
 
 def finish_kernel(*refs):
@@ -201,7 +282,6 @@
         finish_kernel,
         out_shape=[shape, shape],
         compiler_params=room(own, own, *arrived),
-        name="finish",
     )(own, *arrived)
 
 
@@ -228,7 +308,6 @@
         ),
         out_shape=[jax.ShapeDtypeStruct(shape, BF16)] * 2,
         compiler_params=room(*parts, *parts),
-        name="arrange",
     )(ids, *parts)
 
 
@@ -255,7 +334,6 @@
         out_shape=jax.ShapeDtypeStruct((8, HD), jnp.int32),
         cost_estimate=pl.CostEstimate(flops=10**9, bytes_accessed=24 * 2**20, transcendentals=0),
         compiler_params=pltpu.CompilerParams(vmem_limit_bytes=2**20),
-        name="tick",
     )(ids)
 
 
@@ -276,7 +354,6 @@
         append_kernel,
         out_shape=[jax.ShapeDtypeStruct(s, first.dtype) for s in shapes],
         compiler_params=room(first, second, first, second, first, second),
-        name="append",
     )(first, second)
 
 
@@ -285,7 +362,6 @@
         facts_kernel,
         out_shape=jax.ShapeDtypeStruct((1, pooled.shape[1] + texts.size), BF16),
         compiler_params=pltpu.CompilerParams(vmem_limit_bytes=2 * 2**20),
-        name="join_facts",
     )(pooled, texts)
 
 
@@ -330,7 +406,6 @@
         ),
         out_shape=jax.ShapeDtypeStruct((count, n_dp * captions + 2), F32),
         compiler_params=room(*facts, w_proj, facts[0], facts[0], facts[0]),
-        name="similarity_terms",
     )(ids, *facts, w_proj)
 
 
@@ -399,7 +474,6 @@
         ),
         out_shape=jax.ShapeDtypeStruct((2, captions), F32),
         compiler_params=room(*terms),
-        name="losses",
     )(ids, inv_temp, *terms)
 
 
@@ -421,20 +495,18 @@
             rule = lambda z, s=s: lax.rem(z + (n_mp - s), n_mp)
             rest.append([([lax.ppermute(tokens, "mp", pairs)], first, rule)])
         return [[own], *rest]
-    right = lax.ppermute(tokens, "mp", [(0, 1), (1, 2), (2, 3)])
-    left = lax.ppermute(tokens, "mp", [(1, 0), (2, 1), (3, 2)])
+    inner = lambda z: ((z == 1) | (z == 2)).astype(jnp.int32)
+    near = flip(tokens, "mp", n_mp, 1)
+    cross = lax.ppermute(tokens, "mp", [(1, 2), (2, 1)])
     far = lax.ppermute(tokens, "mp", [(0, 3), (3, 0)])
-    right_on = lax.ppermute(right, "mp", [(1, 2), (2, 3)])
-    left_on = lax.ppermute(left, "mp", [(1, 0), (2, 1)])
-    inner = lambda z: (z == 1) | (z == 2)
-    near = ([left, right], lambda z: z & 1, lambda z: z ^ 1)
-    other = (
-        [far, left, right],
-        lambda z: jnp.where(inner(z), z, 0),
-        lambda z: z ^ 3,
-    )
-    last = ([left_on, right_on], lambda z: z >> 1, lambda z: z ^ 2)
-    return [[own], [near], [other], [last]]
+    cross_on = lax.ppermute(cross, "mp", [(2, 3), (1, 0)])
+    near_on = lax.ppermute(near, "mp", [(1, 2), (2, 1)])
+    return [
+        [own],
+        [([near], first, lambda z: z ^ 1)],
+        [([far, cross], inner, lambda z: z ^ 3)],
+        [([cross_on, near_on], inner, lambda z: z ^ 2)],
+    ]
 
 
 def work(
@@ -479,14 +551,12 @@
     half = n_dp // 2
     early = early_terms(turned[:-1] + others[:-1], grads[:-1] + other_grads[:-1])
     sides = (turned[-1:] + others[-1:], grads[-1:] + other_grads[-1:], early)
-    (last,) = weight_terms(ids, (half - 1,), *sides)
-    arrived = [flip(last, "dp", n_dp, 2 * (half - 1))]
-    pieces = weight_terms(ids, tuple(range(half - 2, -1, -1)), *sides)
-    for m, piece in zip(range(half - 2, 0, -1), pieces):
-        arrived.append(flip(piece, "dp", n_dp, 2 * m))
+    if half == 4:
+        dw_key, dw_value = staged_sums(ids, n_dp, sides)
+    else:
+        dw_key, dw_value = direct_sums(ids, n_dp, sides)
     rules = [m[2] for members in groups for m in members]
     attended, grad_queries = arrange(ids, rules, parts, [len(m) for m in groups])
-    dw_key, dw_value = finish(pieces[-1], arrived)
 
     (pooled,) = pooled
     pools = [facts] + [flip(pooled, "mp", n_mp, m) for m in range(1, n_mp)]

time: 89.7 us -> 82.6 us (0.921)
  starting transfers between devices: 36.1 us -> 30 us
  waiting for transfers between devices: 34.8 us -> 33 us
    ppermute x4 -> x3, starting transfers between devices: 8.86 us -> 2.65 us  [the longest x1 1.29 us: gather_images(): cross_on = lax.ppermute(cross, 'mp', [(2, 3), (1, 0)])]
    ppermute x4 -> x3, waiting for transfers between devices: 7.9 us -> 3.35 us  [the longest x1 3.34 us: gather_images(): cross_on = lax.ppermute(cross, 'mp', [(2, 3), (1, 0)])]
    ppermute x20 -> x22, waiting for transfers between devices: 24.3 us -> 26.6 us  [flip(): return lax.ppermute(array, axis, [(n, n ^ mask) for n in range(count)])]
    pallas_call x3 -> x6, Pallas kernels: 2.73 us -> 3.46 us  [the longest x2 1.82 us: term_parts(): pl.pallas_call(functools.partial(part_kernel, len(turned), wanted), grid_...]
    ppermute x20 -> x22, starting transfers between devices: 23.4 us -> 24.1 us  [flip(): return lax.ppermute(array, axis, [(n, n ^ mask) for n in range(count)])]
  transfers between devices with their start and end apart: 25 -> 26, of which waited for: 13 -> 11; matrix products, arithmetic and copies ran while one was open for 0% -> 0% of each run, Pallas kernels for 16% -> 18%
where the time goes in v2:
time: 82.6 us; the launch traced here: 82.4 us
  waiting for transfers between devices  33 us (40%)
  starting transfers between devices  30 us (36%)
  Pallas kernels  16.3 us (20%)
  between operations  1.54 us (2%)
  local copies, waits for them, and re-layouts  1.38 us (2%)
    ppermute x22, waiting for transfers between devices, flip(): return lax.ppermute(array, axis, [(n, n ^ mask) for n in range(count)])  26.6 us
    ppermute x22, starting transfers between devices, flip(): return lax.ppermute(array, axis, [(n, n ^ mask) for n in range(count)])  24.1 us
    pallas_call x4, Pallas kernels, image_group(): pl.pallas_call(functools.partial(group_kernel, width // HD, [len(c) for c...  7.26 us
    ppermute x1, waiting for transfers between devices, gather_images(): cross_on = lax.ppermute(cross, 'mp', [(2, 3), (1, 0)])  3.34 us
    ppermute x1, starting transfers between devices, gather_images(): far = lax.ppermute(tokens, 'mp', [(0, 3), (3, 0)])  3.25 us
    ppermute x1, waiting for transfers between devices, gather_images(): far = lax.ppermute(tokens, 'mp', [(0, 3), (3, 0)])  3.1 us
    pallas_call x2, Pallas kernels, term_parts(): pl.pallas_call(functools.partial(part_kernel, len(turned), wanted), grid_...  1.82 us
  transfers between devices with their start and end apart: 26, of which 11 were waited for; matrix products, arithmetic and copies ran while one was open for 0% of the time, Pallas kernels for 18%

profile of v2, /device:TPU:0, one launch (start us, length us, event | category | flops | bytes accessed | tf_op | source)
XLA Modules:
  0.0 82.4 jit_solution(6106759513288301542)
XLA Ops:
  1.3 5.9 %collective-permute-start = (bf16[1,128,1408]{2,1,0:T(8,128)(2,1)}, bf16[1,128,1408]{2,1,0:T(8,128)(2,1)S(1)}, u32[]{:S(2)}, u32[]{:S(2)}) collective-permute-start(bf16[1,128,1408]{2,1,0:T(8,128)(2,1)} %refs_0_.2), channel_id=1, source_target_pairs={{0,1},{1,0},{2,3},{3,2},{4,5},{5,4},{6,7},{7,6},{8,9},{9,8},{10,11... | collective-permute-start | bytes 1081352 | tf_op jit(solution)/shard_map/ppermute | solution.py:481
  7.2 3.2 %collective-permute-start.1 = (bf16[1,128,1408]{2,1,0:T(8,128)(2,1)}, bf16[1,128,1408]{2,1,0:T(8,128)(2,1)S(1)}, u32[]{:S(2)}, u32[]{:S(2)}) collective-permute-start(bf16[1,128,1408]{2,1,0:T(8,128)(2,1)} %refs_0_.2), channel_id=1, source_target_pairs={{0,3},{3,0},{4,7},{7,4},{8,11},{11,8},{12,15},{15,12},{16,19},{19,... | collective-permute-start | bytes 1081352 | tf_op jit(solution)/shard_map/ppermute | solution.py:501
  10.5 1.3 %collective-permute-start.3 = (bf16[1,128,1408]{2,1,0:T(8,128)(2,1)S(1)}, bf16[1,128,1408]{2,1,0:T(8,128)(2,1)S(1)}, u32[]{:S(2)}, u32[]{:S(2)}) collective-permute-start(bf16[1,128,1408]{2,1,0:T(8,128)(2,1)S(1)} %collective-permute-done.2.refs_1_), channel_id=1, source_target_pairs={{2,3},{1,0},{6,7},{5,4},{10,11},{9,8},{14,15},{13,12},{18,19},{17,... | collective-permute-start | bytes 1081352 | tf_op jit(solution)/shard_map/ppermute | solution.py:502
  11.8 4.5 %collective-permute-done.refs_0_ = bf16[1,128,1408]{2,1,0:T(8,128)(2,1)S(1)} collective-permute-done((bf16[1,128,1408]{2,1,0:T(8,128)(2,1)}, bf16[1,128,1408]{2,1,0:T(8,128)(2,1)S(1)}, u32[]{:S(2)}, u32[]{:S(2)}) %collective-permute-start) | collective-permute-done | bytes 360480 | tf_op jit(solution)/shard_map/ppermute | solution.py:481
  19.0 1.8 %shard_map.138 = (bf16[1,32,512]{2,1,0:T(8,128)(2,1)S(1)}, bf16[1,32,512]{2,1,0:T(8,128)(2,1)S(1)}, bf16[128,1024]{1,0:T(8,128)(2,1)S(1)}, bf16[1,4,176,128]{3,2...) custom-call(s32[2]{0:T(128)S(1)} %pad_add_fusion.ids, s32[4]{0:T(128)S(1)} %copy-done.6, bf16[1,128,1408]{2,1,0:T(8,128)(2,1)S(1)} %copy-done.5, ...), custom_call_target="tpu_custom_call" | custom-call | tf_op jit(solution)/shard_map/pallas_call | solution.py:108
  21.4 3.1 %collective-permute-done.1.refs_0_ = bf16[1,128,1408]{2,1,0:T(8,128)(2,1)S(1)} collective-permute-done((bf16[1,128,1408]{2,1,0:T(8,128)(2,1)}, bf16[1,128,1408]{2,1,0:T(8,128)(2,1)S(1)}, u32[]{:S(2)}, u32[]{:S(2)}) %collective-permute-start.1) | collective-permute-done | bytes 360480 | tf_op jit(solution)/shard_map/ppermute | solution.py:501
  24.5 1.8 %shard_map.140 = (bf16[1,32,512]{2,1,0:T(8,128)(2,1)S(1)}, bf16[1,32,512]{2,1,0:T(8,128)(2,1)S(1)}, bf16[128,1024]{1,0:T(8,128)(2,1)S(1)}, bf16[1,4,176,128]{3,2...) custom-call(s32[2]{0:T(128)S(1)} %pad_add_fusion.ids, s32[4]{0:T(128)S(1)} %copy-done.6, ...), custom_call_target="tpu_custom_call" | custom-call | tf_op jit(solution)/shard_map/pallas_call | solution.py:108
  26.4 1.8 %shard_map.139 = (bf16[1,32,512]{2,1,0:T(8,128)(2,1)S(1)}, bf16[1,32,512]{2,1,0:T(8,128)(2,1)S(1)}, bf16[128,1024]{1,0:T(8,128)(2,1)S(1)}, bf16[1,4,176,128]{3,2...) custom-call(s32[2]{0:T(128)S(1)} %pad_add_fusion.ids, s32[4]{0:T(128)S(1)} %copy-done.6, ...), custom_call_target="tpu_custom_call" | custom-call | tf_op jit(solution)/shard_map/pallas_call | solution.py:108
  28.2 3.3 %collective-permute-done.3.refs_0_ = bf16[1,128,1408]{2,1,0:T(8,128)(2,1)S(1)} collective-permute-done((bf16[1,128,1408]{2,1,0:T(8,128)(2,1)S(1)}, bf16[1,128,1408]{2,1,0:T(8,128)(2,1)S(1)}, u32[]{:S(2)}, u32[]{:S(2)}) %collective-permute-start.3) | collective-permute-done | bytes 360480 | tf_op jit(solution)/shard_map/ppermute | solution.py:502
  32.1 1.8 %shard_map.141 = (bf16[1,32,512]{2,1,0:T(8,128)(2,1)S(1)}, bf16[1,32,512]{2,1,0:T(8,128)(2,1)S(1)}, bf16[128,1024]{1,0:T(8,128)(2,1)S(1)}, bf16[1,4,176,128]{3,2...) custom-call(s32[2]{0:T(128)S(1)} %pad_add_fusion.ids, s32[4]{0:T(128)S(1)} %copy-done.6, ...), custom_call_target="tpu_custom_call" | custom-call | tf_op jit(solution)/shard_map/pallas_call | solution.py:108
  34.6 1.2 %collective-permute-done.8.refs_4_ = bf16[1,4,176,128]{3,2,1,0:T(8,128)(2,1)S(1)} collective-permute-done((bf16[1,4,176,128]{3,2,1,0:T(8,128)(2,1)S(1)}, bf16[1,4,176,128]{3,2,1,0:T(8,128)(2,1)S(1)}, u32[]{:S(2)}, u32[]{:S(2)}) %collective-permute-start.8) | collective-permute-done | bytes 180256 | tf_op jit(solution)/shard_map/ppermute | solution.py:481
  35.8 1.3 %shard_map.143.refs_4_ = f32[4,176,1024]{2,1,0:T(8,128)S(1)} custom-call(bf16[1,4,176,128]{3,2,1,0:T(8,128)(2,1)S(1)} %get-tuple-element.46.refs_0_, bf16[1,4,176,128]{3,2,1,0:T(8,128)(2,1)S(1)} %get-tuple-element.47.refs_1_, bf16[1,4,176,128]{3,2,1,0:T(8,128)(2,1)S(1)} %get-tuple-element.48.refs_2_, ...), custom_call_target="tpu_custom_call" | custom-call | tf_op jit(solution)/shard_map/pallas_call | solution.py:141
  37.2 0.9 %shard_map.145 = (bf16[2,176,512]{2,1,0:T(8,128)(2,1)S(1)}, bf16[2,176,512]{2,1,0:T(8,128)(2,1)S(1)}) custom-call(s32[2]{0:T(128)S(1)} %pad_add_fusion.ids, bf16[1,4,176,128]{3,2,1,0:T(8,128)(2,1)S(1)} %get-tuple-element.43.refs_0_, bf16[1,4,176,128]{3,2,1,0:T(8,128)(2,1)S(1)} %collective-permute-done.5.refs_1_, ...), custom_call_target="tpu_custom_call" | custom-call | tf_op jit(solution)/shard_map/pallas_call | solution.py:207
  38.1 1.6 %collective-permute-start.15 = (bf16[2,176,512]{2,1,0:T(8,128)(2,1)S(1)}, bf16[2,176,512]{2,1,0:T(8,128)(2,1)S(1)}, u32[]{:S(2)}, u32[]{:S(2)}) collective-permute-start(bf16[2,176,512]{2,1,0:T(8,128)(2,1)S(1)} %get-tuple-element.58), channel_id=1, source_target_pairs={{0,16},{4,20},{8,24},{12,28},{16,0},{20,4},{24,8},{28,12},{1,17},{... | collective-permute-start | bytes 1081352 | tf_op jit(solution)/shard_map/ppermute | solution.py:481
  39.7 1.5 %collective-permute-start.13 = (bf16[2,176,512]{2,1,0:T(8,128)(2,1)S(1)}, bf16[2,176,512]{2,1,0:T(8,128)(2,1)S(1)}, u32[]{:S(2)}, u32[]{:S(2)}) collective-permute-start(bf16[2,176,512]{2,1,0:T(8,128)(2,1)S(1)} %get-tuple-element.56), channel_id=1, source_target_pairs={{0,8},{4,12},{8,0},{12,4},{16,24},{20,28},{24,16},{28,20},{1,9},{5... | collective-permute-start | bytes 1081352 | tf_op jit(solution)/shard_map/ppermute | solution.py:481
  42.1 6.5 %collective-permute-done.15.got.first = bf16[2,176,512]{2,1,0:T(8,128)(2,1)S(1)} collective-permute-done((bf16[2,176,512]{2,1,0:T(8,128)(2,1)S(1)}, bf16[2,176,512]{2,1,0:T(8,128)(2,1)S(1)}, u32[]{:S(2)}, u32[]{:S(2)}) %collective-permute-start.15) | collective-permute-done | bytes 360480 | tf_op jit(solution)/shard_map/ppermute | solution.py:481
  48.6 1.6 %collective-permute-start.16 = (bf16[176,512]{1,0:T(8,128)(2,1)S(1)}, bf16[176,512]{1,0:T(8,128)(2,1)S(1)}, u32[]{:S(2)}, u32[]{:S(2)}) collective-permute-start(bf16[176,512]{1,0:T(8,128)(2,1)S(1)} %shard_map.148), channel_id=1, source_target_pairs={{0,8},{4,12},{8,0},{12,4},{16,24},{20,28},{24,16},{28,20},{1,9},{5... | collective-permute-start | bytes 540680 | tf_op jit(solution)/shard_map/ppermute | solution.py:481
  50.2 1.6 %collective-permute-start.14 = (bf16[176,512]{1,0:T(8,128)(2,1)S(1)}, bf16[176,512]{1,0:T(8,128)(2,1)S(1)}, u32[]{:S(2)}, u32[]{:S(2)}) collective-permute-start(bf16[176,512]{1,0:T(8,128)(2,1)S(1)} %shard_map.146), channel_id=1, source_target_pairs={{0,16},{4,20},{8,24},{12,28},{16,0},{20,4},{24,8},{28,12},{1,17},{... | collective-permute-start | bytes 540680 | tf_op jit(solution)/shard_map/ppermute | solution.py:481
  51.9 1.2 %collective-permute-done.17.second = bf16[1,3456]{1,0:T(2,128)(2,1)S(1)} collective-permute-done((bf16[1,3456]{1,0:T(2,128)(2,1)S(1)}, bf16[1,3456]{1,0:T(2,128)(2,1)S(1)}, u32[]{:S(2)}, u32[]{:S(2)}) %collective-permute-start.17) | collective-permute-done | bytes 6944 | tf_op jit(solution)/shard_map/ppermute | solution.py:481
  53.7 3.1 %collective-permute-done.18.second = bf16[2,3456]{1,0:T(2,128)(2,1)S(1)} collective-permute-done((bf16[2,3456]{1,0:T(2,128)(2,1)S(1)}, bf16[2,3456]{1,0:T(2,128)(2,1)S(1)}, u32[]{:S(2)}, u32[]{:S(2)}) %collective-permute-start.18) | collective-permute-done | bytes 13856 | tf_op jit(solution)/shard_map/ppermute | solution.py:481
  57.5 3.3 %collective-permute-done.19.second = bf16[4,3456]{1,0:T(4,128)(2,1)S(1)} collective-permute-done((bf16[4,3456]{1,0:T(4,128)(2,1)S(1)}, bf16[4,3456]{1,0:T(4,128)(2,1)S(1)}, u32[]{:S(2)}, u32[]{:S(2)}) %collective-permute-start.19) | collective-permute-done | bytes 27680 | tf_op jit(solution)/shard_map/ppermute | solution.py:481
  60.8 1.0 %collective-permute-start.20 = (bf16[8,1408]{1,0:T(8,128)(2,1)S(1)}, bf16[8,1408]{1,0:T(8,128)(2,1)S(1)}, u32[]{:S(2)}, u32[]{:S(2)}) collective-permute-start(bf16[8,1408]{1,0:T(8,128)(2,1)S(1)} %get-tuple-element.60), channel_id=1, source_target_pairs={{0,1},{1,0},{2,3},{3,2},{4,5},{5,4},{6,7},{7,6},{8,9},{9,8},{10,11... | collective-permute-start | bytes 67592 | tf_op jit(solution)/shard_map/ppermute | solution.py:481
  61.9 2.1 %collective-permute-start.21 = (bf16[8,1408]{1,0:T(8,128)(2,1)S(1)}, bf16[8,1408]{1,0:T(8,128)(2,1)S(1)}, u32[]{:S(2)}, u32[]{:S(2)}) collective-permute-start(bf16[8,1408]{1,0:T(8,128)(2,1)S(1)} %get-tuple-element.60), channel_id=1, source_target_pairs={{0,2},{1,3},{2,0},{3,1},{4,6},{5,7},{6,4},{7,5},{8,10},{9,11},{10,... | collective-permute-start | bytes 67592 | tf_op jit(solution)/shard_map/ppermute | solution.py:481
  64.0 1.3 %collective-permute-start.22 = (bf16[8,1408]{1,0:T(8,128)(2,1)S(1)}, bf16[8,1408]{1,0:T(8,128)(2,1)S(1)}, u32[]{:S(2)}, u32[]{:S(2)}) collective-permute-start(bf16[8,1408]{1,0:T(8,128)(2,1)S(1)} %get-tuple-element.60), channel_id=1, source_target_pairs={{0,3},{1,2},{2,1},{3,0},{4,7},{5,6},{6,5},{7,4},{8,11},{9,10},{10,... | collective-permute-start | bytes 67592 | tf_op jit(solution)/shard_map/ppermute | solution.py:481
  65.3 1.3 %collective-permute-done.21.refs_2_ = bf16[8,1408]{1,0:T(8,128)(2,1)S(1)} collective-permute-done((bf16[8,1408]{1,0:T(8,128)(2,1)S(1)}, bf16[8,1408]{1,0:T(8,128)(2,1)S(1)}, u32[]{:S(2)}, u32[]{:S(2)}) %collective-permute-start.21) | collective-permute-done | bytes 22560 | tf_op jit(solution)/shard_map/ppermute | solution.py:481
  66.6 3.0 %collective-permute-done.22.refs_3_ = bf16[8,1408]{1,0:T(8,128)(2,1)S(1)} collective-permute-done((bf16[8,1408]{1,0:T(8,128)(2,1)S(1)}, bf16[8,1408]{1,0:T(8,128)(2,1)S(1)}, u32[]{:S(2)}, u32[]{:S(2)}) %collective-permute-start.22) | collective-permute-done | bytes 22560 | tf_op jit(solution)/shard_map/ppermute | solution.py:481
  69.6 1.0 %shard_map.154.refs_1_ = f32[32,34]{1,0:T(8,128)S(1)} custom-call(s32[2]{0:T(128)S(1)} %pad_add_fusion.ids, bf16[8,3456]{1,0:T(8,128)(2,1)S(1)} %get-tuple-element.59.refs_0_, bf16[8,1408]{1,0:T(8,128)(2,1)S(1)} %collective-permute-done.20.refs_1_, bf16[8,1408]{1,0:T(8,128)(2,1)S(1)} %collective-permute-done.21.refs_2_, ...), custom_call_target="tpu_custom_call" | custom-call | tf_op jit(solution)/shard_map/pallas_call | solution.py:395
  70.7 1.9 %collective-permute-start.24 = (f32[32,34]{1,0:T(8,128)S(1)}, f32[32,34]{1,0:T(8,128)S(1)}, u32[]{:S(2)}, u32[]{:S(2)}) collective-permute-start(f32[32,34]{1,0:T(8,128)S(1)} %shard_map.154.refs_1_), channel_id=1, source_target_pairs={{0,2},{1,3},{2,0},{3,1},{4,6},{5,7},{6,4},{7,5},{8,10},{9,11},{10,... | collective-permute-start | bytes 13064 | tf_op jit(solution)/shard_map/ppermute | solution.py:481
  72.5 2.5 %collective-permute-start.25 = (f32[32,34]{1,0:T(8,128)S(1)}, f32[32,34]{1,0:T(8,128)S(1)}, u32[]{:S(2)}, u32[]{:S(2)}) collective-permute-start(f32[32,34]{1,0:T(8,128)S(1)} %shard_map.154.refs_1_), channel_id=1, source_target_pairs={{0,3},{1,2},{2,1},{3,0},{4,7},{5,6},{6,5},{7,4},{8,11},{9,10},{10,... | collective-permute-start | bytes 13064 | tf_op jit(solution)/shard_map/ppermute | solution.py:481
  75.7 2.4 %collective-permute-done.25.refs_4_ = f32[32,34]{1,0:T(8,128)S(1)} collective-permute-done((f32[32,34]{1,0:T(8,128)S(1)}, f32[32,34]{1,0:T(8,128)S(1)}, u32[]{:S(2)}, u32[]{:S(2)}) %collective-permute-start.25) | collective-permute-done | bytes 4384 | tf_op jit(solution)/shard_map/ppermute | solution.py:481
  78.1 1.4 %shard_map.155 = f32[2,4]{1,0:T(2,128)} custom-call(s32[2]{0:T(128)S(1)} %pad_add_fusion.ids, f32[1]{0:T(128)S(6)} %copy.15.refs_0_, f32[32,34]{1,0:T(8,128)S(1)} %shard_map.154.refs_1_, f32[32,34]{1,0:T(8,128)S(1)} %collective-permute-done.23.refs_2_, f32[32,34]{1,0:T(8,128)S(1)} %collective-permute-done.24.refs_3_, ...), custom_call_target="tpu_custom_call" | custom-call | tf_op jit(solution)/shard_map/pallas_call | solution.py:466
  79.5 1.3 %shard_map.142 = (bf16[4,32,512]{2,1,0:T(8,128)(2,1)}, bf16[4,32,512]{2,1,0:T(8,128)(2,1)}) custom-call(s32[2]{0:T(128)S(1)} %pad_add_fusion.ids, bf16[1,32,512]{2,1,0:T(8,128)(2,1)S(1)} %get-tuple-element.33.refs_0_, bf16[1,32,512]{2,1,0:T(8,128)(2,1)S(1)} %get-tuple-element.34.refs_1_, bf16[1,32,512]{2,1,0:T(8,128)(2,1)S(1)} %get-tuple-element.35.refs_2_, ...), custom_call_target="tpu_custom_call" | custom-call | tf_op jit(solution)/shard_map/pallas_call | solution.py:301
  (58 shorter events, 9.2 us)
Async XLA Ops:
  0.6 9.9 %collective-permute-start.2 = (bf16[1,128,1408]{2,1,0:T(8,128)(2,1)}, bf16[1,128,1408]{2,1,0:T(8,128)(2,1)S(1)}, u32[]{:S(2)}, u32[]{:S(2)}) collective-permute-start(bf16[1,128,1408]{2,1,0:T(8,128)(2,1)} %refs_0_.2), channel_id=1, source_target_pairs={{1,2},{2,1},{5,6},{6,5},{9,10},{10,9},{13,14},{14,13},{17,18},{18,... | collective-permute-start | bytes 1081352 | tf_op jit(solution)/shard_map/ppermute | solution.py:500
  1.3 15.0 %collective-permute-start = (bf16[1,128,1408]{2,1,0:T(8,128)(2,1)}, bf16[1,128,1408]{2,1,0:T(8,128)(2,1)S(1)}, u32[]{:S(2)}, u32[]{:S(2)}) collective-permute-start(bf16[1,128,1408]{2,1,0:T(8,128)(2,1)} %refs_0_.2), channel_id=1, source_target_pairs={{0,1},{1,0},{2,3},{3,2},{4,5},{5,4},{6,7},{7,6},{8,9},{9,8},{10,11... | collective-permute-start | bytes 1081352 | tf_op jit(solution)/shard_map/ppermute | solution.py:481
  7.2 17.3 %collective-permute-start.1 = (bf16[1,128,1408]{2,1,0:T(8,128)(2,1)}, bf16[1,128,1408]{2,1,0:T(8,128)(2,1)S(1)}, u32[]{:S(2)}, u32[]{:S(2)}) collective-permute-start(bf16[1,128,1408]{2,1,0:T(8,128)(2,1)} %refs_0_.2), channel_id=1, source_target_pairs={{0,3},{3,0},{4,7},{7,4},{8,11},{11,8},{12,15},{15,12},{16,19},{19,... | collective-permute-start | bytes 1081352 | tf_op jit(solution)/shard_map/ppermute | solution.py:501
  10.5 21.1 %collective-permute-start.3 = (bf16[1,128,1408]{2,1,0:T(8,128)(2,1)S(1)}, bf16[1,128,1408]{2,1,0:T(8,128)(2,1)S(1)}, u32[]{:S(2)}, u32[]{:S(2)}) collective-permute-start(bf16[1,128,1408]{2,1,0:T(8,128)(2,1)S(1)} %collective-permute-done.2.refs_1_), channel_id=1, source_target_pairs={{2,3},{1,0},{6,7},{5,4},{10,11},{9,8},{14,15},{13,12},{18,19},{17,... | collective-permute-start | bytes 1081352 | tf_op jit(solution)/shard_map/ppermute | solution.py:502
  16.4 15.2 %collective-permute-start.4 = (bf16[1,128,1408]{2,1,0:T(8,128)(2,1)S(1)}, bf16[1,128,1408]{2,1,0:T(8,128)(2,1)S(1)}, u32[]{:S(2)}, u32[]{:S(2)}) collective-permute-start(bf16[1,128,1408]{2,1,0:T(8,128)(2,1)S(1)} %collective-permute-done.refs_0_), channel_id=1, source_target_pairs={{1,2},{2,1},{5,6},{6,5},{9,10},{10,9},{13,14},{14,13},{17,18},{18,... | collective-permute-start | bytes 1081352 | tf_op jit(solution)/shard_map/ppermute | solution.py:503
  17.1 1.8 %copy-start.3 = (bf16[4,32,512]{2,1,0:T(8,128)(2,1)S(1)}, bf16[4,32,512]{2,1,0:T(8,128)(2,1)}, u32[]{:S(2)}) copy-start(bf16[4,32,512]{2,1,0:T(8,128)(2,1)} %refs_6_.3) | copy-start | bytes 393220
  17.1 1.9 %copy-start.5 = (bf16[1,128,1408]{2,1,0:T(8,128)(2,1)S(1)}, bf16[1,128,1408]{2,1,0:T(8,128)(2,1)}, u32[]{:S(2)}) copy-start(bf16[1,128,1408]{2,1,0:T(8,128)(2,1)} %refs_0_.2) | copy-start | bytes 1081348
  17.1 1.9 %copy-start.6 = (s32[4]{0:T(128)S(1)}, s32[4]{0:T(128)}, u32[]{:S(2)}) copy-start(s32[4]{0:T(128)} %lens.7) | copy-start | bytes 52
  20.8 13.2 %collective-permute-start.10 = (bf16[128,1024]{1,0:T(8,128)(2,1)S(1)}, bf16[128,1024]{1,0:T(8,128)(2,1)S(1)}, u32[]{:S(2)}, u32[]{:S(2)}) collective-permute-start(bf16[128,1024]{1,0:T(8,128)(2,1)S(1)} %get-tuple-element.52.refs_6_), channel_id=1, source_target_pairs={{0,4},{4,0},{8,12},{12,8},{16,20},{20,16},{24,28},{28,24},{1,5},{5... | collective-permute-start | bytes 786440 | tf_op jit(solution)/shard_map/ppermute | solution.py:481
  20.9 13.0 %collective-permute-start.7 = (bf16[1,4,176,128]{3,2,1,0:T(8,128)(2,1)S(1)}, bf16[1,4,176,128]{3,2,1,0:T(8,128)(2,1)S(1)}, u32[]{:S(2)}, u32[]{:S(2)}) collective-permute-start(bf16[1,4,176,128]{3,2,1,0:T(8,128)(2,1)S(1)} %get-tuple-element.49), channel_id=1, source_target_pairs={{0,4},{4,0},{8,12},{12,8},{16,20},{20,16},{24,28},{28,24},{1,5},{5... | collective-permute-start | bytes 540680 | tf_op jit(solution)/shard_map/ppermute | solution.py:481
  26.4 8.2 %collective-permute-start.9 = (bf16[1,4,176,128]{3,2,1,0:T(8,128)(2,1)S(1)}, bf16[1,4,176,128]{3,2,1,0:T(8,128)(2,1)S(1)}, u32[]{:S(2)}, u32[]{:S(2)}) collective-permute-start(bf16[1,4,176,128]{3,2,1,0:T(8,128)(2,1)S(1)} %get-tuple-element.51), channel_id=1, source_target_pairs={{0,4},{4,0},{8,12},{12,8},{16,20},{20,16},{24,28},{28,24},{1,5},{5... | collective-permute-start | bytes 540680 | tf_op jit(solution)/shard_map/ppermute | solution.py:481
  31.6 4.2 %collective-permute-start.12 = (bf16[128,1024]{1,0:T(8,128)(2,1)S(1)}, bf16[128,1024]{1,0:T(8,128)(2,1)S(1)}, u32[]{:S(2)}, u32[]{:S(2)}) collective-permute-start(bf16[128,1024]{1,0:T(8,128)(2,1)S(1)} %get-tuple-element.54.refs_8_), channel_id=1, source_target_pairs={{0,4},{4,0},{8,12},{12,8},{16,20},{20,16},{24,28},{28,24},{1,5},{5... | collective-permute-start | bytes 786440 | tf_op jit(solution)/shard_map/ppermute | solution.py:481
  31.6 4.2 %collective-permute-start.11 = (bf16[128,1024]{1,0:T(8,128)(2,1)S(1)}, bf16[128,1024]{1,0:T(8,128)(2,1)S(1)}, u32[]{:S(2)}, u32[]{:S(2)}) collective-permute-start(bf16[128,1024]{1,0:T(8,128)(2,1)S(1)} %get-tuple-element.53.refs_7_), channel_id=1, source_target_pairs={{0,4},{4,0},{8,12},{12,8},{16,20},{20,16},{24,28},{28,24},{1,5},{5... | collective-permute-start | bytes 786440 | tf_op jit(solution)/shard_map/ppermute | solution.py:481
  33.9 3.2 %collective-permute-start.6 = (bf16[128,1024]{1,0:T(8,128)(2,1)S(1)}, bf16[128,1024]{1,0:T(8,128)(2,1)S(1)}, u32[]{:S(2)}, u32[]{:S(2)}) collective-permute-start(bf16[128,1024]{1,0:T(8,128)(2,1)S(1)} %get-tuple-element.45.refs_2_), channel_id=1, source_target_pairs={{0,4},{4,0},{8,12},{12,8},{16,20},{20,16},{24,28},{28,24},{1,5},{5... | collective-permute-start | bytes 786440 | tf_op jit(solution)/shard_map/ppermute | solution.py:481
  34.0 1.8 %collective-permute-start.8 = (bf16[1,4,176,128]{3,2,1,0:T(8,128)(2,1)S(1)}, bf16[1,4,176,128]{3,2,1,0:T(8,128)(2,1)S(1)}, u32[]{:S(2)}, u32[]{:S(2)}) collective-permute-start(bf16[1,4,176,128]{3,2,1,0:T(8,128)(2,1)S(1)} %get-tuple-element.50), channel_id=1, source_target_pairs={{0,4},{4,0},{8,12},{12,8},{16,20},{20,16},{24,28},{28,24},{1,5},{5... | collective-permute-start | bytes 540680 | tf_op jit(solution)/shard_map/ppermute | solution.py:481
  34.5 2.6 %collective-permute-start.5 = (bf16[1,4,176,128]{3,2,1,0:T(8,128)(2,1)S(1)}, bf16[1,4,176,128]{3,2,1,0:T(8,128)(2,1)S(1)}, u32[]{:S(2)}, u32[]{:S(2)}) collective-permute-start(bf16[1,4,176,128]{3,2,1,0:T(8,128)(2,1)S(1)} %get-tuple-element.44), channel_id=1, source_target_pairs={{0,4},{4,0},{8,12},{12,8},{16,20},{20,16},{24,28},{28,24},{1,5},{5... | collective-permute-start | bytes 540680 | tf_op jit(solution)/shard_map/ppermute | solution.py:481
  38.1 10.5 %collective-permute-start.15 = (bf16[2,176,512]{2,1,0:T(8,128)(2,1)S(1)}, bf16[2,176,512]{2,1,0:T(8,128)(2,1)S(1)}, u32[]{:S(2)}, u32[]{:S(2)}) collective-permute-start(bf16[2,176,512]{2,1,0:T(8,128)(2,1)S(1)} %get-tuple-element.58), channel_id=1, source_target_pairs={{0,16},{4,20},{8,24},{12,28},{16,0},{20,4},{24,8},{28,12},{1,17},{... | collective-permute-start | bytes 1081352 | tf_op jit(solution)/shard_map/ppermute | solution.py:481
  39.7 10.5 %collective-permute-start.13 = (bf16[2,176,512]{2,1,0:T(8,128)(2,1)S(1)}, bf16[2,176,512]{2,1,0:T(8,128)(2,1)S(1)}, u32[]{:S(2)}, u32[]{:S(2)}) collective-permute-start(bf16[2,176,512]{2,1,0:T(8,128)(2,1)S(1)} %get-tuple-element.56), channel_id=1, source_target_pairs={{0,8},{4,12},{8,0},{12,4},{16,24},{20,28},{24,16},{28,20},{1,9},{5... | collective-permute-start | bytes 1081352 | tf_op jit(solution)/shard_map/ppermute | solution.py:481
  42.1 9.8 %copy-start.7 = (bf16[1,1408]{1,0:T(2,128)(2,1)S(1)}, bf16[1,1408]{1,0:T(2,128)(2,1)}, u32[]{:S(2)}) copy-start(bf16[1,1408]{1,0:T(2,128)(2,1)} %pooled.1) | copy-start | bytes 8452
  42.1 9.8 %copy-start.8 = (bf16[4,512]{1,0:T(4,128)(2,1)S(1)}, bf16[4,512]{1,0:T(4,128)(2,1)}, u32[]{:S(2)}) copy-start(bf16[4,512]{1,0:T(4,128)(2,1)} %texts.1) | copy-start | bytes 12292
  42.1 27.5 %copy-start.4 = (bf16[1408,512]{1,0:T(8,128)(2,1)S(1)}, bf16[1408,512]{1,0:T(8,128)(2,1)}, u32[]{:S(2)}) copy-start(bf16[1408,512]{1,0:T(8,128)(2,1)} %refs_4_.9) | copy-start | bytes 4325380
  48.6 32.1 %collective-permute-start.16 = (bf16[176,512]{1,0:T(8,128)(2,1)S(1)}, bf16[176,512]{1,0:T(8,128)(2,1)S(1)}, u32[]{:S(2)}, u32[]{:S(2)}) collective-permute-start(bf16[176,512]{1,0:T(8,128)(2,1)S(1)} %shard_map.148), channel_id=1, source_target_pairs={{0,8},{4,12},{8,0},{12,4},{16,24},{20,28},{24,16},{28,20},{1,9},{5... | collective-permute-start | bytes 540680 | tf_op jit(solution)/shard_map/ppermute | solution.py:481
  50.2 31.3 %collective-permute-start.14 = (bf16[176,512]{1,0:T(8,128)(2,1)S(1)}, bf16[176,512]{1,0:T(8,128)(2,1)S(1)}, u32[]{:S(2)}, u32[]{:S(2)}) collective-permute-start(bf16[176,512]{1,0:T(8,128)(2,1)S(1)} %shard_map.146), channel_id=1, source_target_pairs={{0,16},{4,20},{8,24},{12,28},{16,0},{20,4},{24,8},{28,12},{1,17},{... | collective-permute-start | bytes 540680 | tf_op jit(solution)/shard_map/ppermute | solution.py:481
  51.8 1.2 %collective-permute-start.17 = (bf16[1,3456]{1,0:T(2,128)(2,1)S(1)}, bf16[1,3456]{1,0:T(2,128)(2,1)S(1)}, u32[]{:S(2)}, u32[]{:S(2)}) collective-permute-start(bf16[1,3456]{1,0:T(2,128)(2,1)S(1)} %shard_map.150.first), channel_id=1, source_target_pairs={{0,4},{4,0},{8,12},{12,8},{16,20},{20,16},{24,28},{28,24},{1,5},{5... | collective-permute-start | bytes 20744 | tf_op jit(solution)/shard_map/ppermute | solution.py:481
  53.1 3.8 %collective-permute-start.18 = (bf16[2,3456]{1,0:T(2,128)(2,1)S(1)}, bf16[2,3456]{1,0:T(2,128)(2,1)S(1)}, u32[]{:S(2)}, u32[]{:S(2)}) collective-permute-start(bf16[2,3456]{1,0:T(2,128)(2,1)S(1)} %shard_map.151.first), channel_id=1, source_target_pairs={{0,8},{4,12},{8,0},{12,4},{16,24},{20,28},{24,16},{28,20},{1,9},{5... | collective-permute-start | bytes 41480 | tf_op jit(solution)/shard_map/ppermute | solution.py:481
  56.9 3.9 %collective-permute-start.19 = (bf16[4,3456]{1,0:T(4,128)(2,1)S(1)}, bf16[4,3456]{1,0:T(4,128)(2,1)S(1)}, u32[]{:S(2)}, u32[]{:S(2)}) collective-permute-start(bf16[4,3456]{1,0:T(4,128)(2,1)S(1)} %shard_map.152.first), channel_id=1, source_target_pairs={{0,16},{4,20},{8,24},{12,28},{16,0},{20,4},{24,8},{28,12},{1,17},{... | collective-permute-start | bytes 82952 | tf_op jit(solution)/shard_map/ppermute | solution.py:481
  60.8 4.5 %collective-permute-start.20 = (bf16[8,1408]{1,0:T(8,128)(2,1)S(1)}, bf16[8,1408]{1,0:T(8,128)(2,1)S(1)}, u32[]{:S(2)}, u32[]{:S(2)}) collective-permute-start(bf16[8,1408]{1,0:T(8,128)(2,1)S(1)} %get-tuple-element.60), channel_id=1, source_target_pairs={{0,1},{1,0},{2,3},{3,2},{4,5},{5,4},{6,7},{7,6},{8,9},{9,8},{10,11... | collective-permute-start | bytes 67592 | tf_op jit(solution)/shard_map/ppermute | solution.py:481
  61.9 4.7 %collective-permute-start.21 = (bf16[8,1408]{1,0:T(8,128)(2,1)S(1)}, bf16[8,1408]{1,0:T(8,128)(2,1)S(1)}, u32[]{:S(2)}, u32[]{:S(2)}) collective-permute-start(bf16[8,1408]{1,0:T(8,128)(2,1)S(1)} %get-tuple-element.60), channel_id=1, source_target_pairs={{0,2},{1,3},{2,0},{3,1},{4,6},{5,7},{6,4},{7,5},{8,10},{9,11},{10,... | collective-permute-start | bytes 67592 | tf_op jit(solution)/shard_map/ppermute | solution.py:481
  64.0 5.6 %collective-permute-start.22 = (bf16[8,1408]{1,0:T(8,128)(2,1)S(1)}, bf16[8,1408]{1,0:T(8,128)(2,1)S(1)}, u32[]{:S(2)}, u32[]{:S(2)}) collective-permute-start(bf16[8,1408]{1,0:T(8,128)(2,1)S(1)} %get-tuple-element.60), channel_id=1, source_target_pairs={{0,3},{1,2},{2,1},{3,0},{4,7},{5,6},{6,5},{7,4},{8,11},{9,10},{10,... | collective-permute-start | bytes 67592 | tf_op jit(solution)/shard_map/ppermute | solution.py:481
  70.6 5.1 %collective-permute-start.23 = (f32[32,34]{1,0:T(8,128)S(1)}, f32[32,34]{1,0:T(8,128)S(1)}, u32[]{:S(2)}, u32[]{:S(2)}) collective-permute-start(f32[32,34]{1,0:T(8,128)S(1)} %shard_map.154.refs_1_), channel_id=1, source_target_pairs={{0,1},{1,0},{2,3},{3,2},{4,5},{5,4},{6,7},{7,6},{8,9},{9,8},{10,11... | collective-permute-start | bytes 13064 | tf_op jit(solution)/shard_map/ppermute | solution.py:481
  70.7 5.0 %collective-permute-start.24 = (f32[32,34]{1,0:T(8,128)S(1)}, f32[32,34]{1,0:T(8,128)S(1)}, u32[]{:S(2)}, u32[]{:S(2)}) collective-permute-start(f32[32,34]{1,0:T(8,128)S(1)} %shard_map.154.refs_1_), channel_id=1, source_target_pairs={{0,2},{1,3},{2,0},{3,1},{4,6},{5,7},{6,4},{7,5},{8,10},{9,11},{10,... | collective-permute-start | bytes 13064 | tf_op jit(solution)/shard_map/ppermute | solution.py:481
  72.5 5.5 %collective-permute-start.25 = (f32[32,34]{1,0:T(8,128)S(1)}, f32[32,34]{1,0:T(8,128)S(1)}, u32[]{:S(2)}, u32[]{:S(2)}) collective-permute-start(f32[32,34]{1,0:T(8,128)S(1)} %shard_map.154.refs_1_), channel_id=1, source_target_pairs={{0,3},{1,2},{2,1},{3,0},{4,7},{5,6},{6,5},{7,4},{8,11},{9,10},{10,... | collective-permute-start | bytes 13064 | tf_op jit(solution)/shard_map/ppermute | solution.py:481
  (3 other events, 5.0 us)
